TPU v7x, 256 devices: a 8x8x2 block of a 8x8x16 slice. The times are simulated.
256 devices in a mesh: grp: 2 (over z), seq: 16 (over y, core), head: 8 (over x).
Axes of the slice: x: 8, y: 8, z: 2, core: 2. Of those that a mesh axis runs over, the one named last changes fastest.
The devices are a block of a 8x8x16 slice.
Arguments:
- q_latent: bfloat16 [32, 128, 512], P(('grp', 'seq'), 'head'), parts along dimension 0, may hold values from -6 to 6
- q_rope: bfloat16 [32, 128, 64], P(('grp', 'seq'), 'head'), parts along dimension 0, may hold values from -6 to 6
- cache_latent: bfloat16 [9216, 128, 512], P(('grp', 'seq', 'head')), parts along dimension 0, may hold values from -6 to 6
- cache_rope: bfloat16 [9216, 64, 128], P(('grp', 'seq', 'head')), parts along dimension 0, may hold values from -6 to 6
- page_table: int32 [32, 512], P(('grp', 'seq')), parts along dimension 0, may hold values from -1 to 4607, as said below
- lengths: int32 [32], P(('grp', 'seq')), parts along dimension 0, may hold values from 1 to 65536, as said below
Outputs:
- attended: bfloat16 [32, 128, 512], P(('grp', 'seq'), 'head'), parts along dimension 0
There are 2 independent parts, one for each index of `grp`. A program takes and returns all parts, laid end to end along the dimension named above; each array names one. Nothing has to cross between parts.
Inputs may be any that keep to these rules, and one draw needn't show every extreme that they name: `page_table`: row s holds the pool slots of the pages of sequence s in page order; entries from ceil(lengths[s] / 128) on are -1; no slot appears twice in the table. Slots d * 36 to (d + 1) * 36 - 1 belong to device d of seq+head (seq index first). One device holds at most 4 pages of one sequence; one sequence has exactly 4 pages on every device. Sequence s has ceil(lengths[s] / 128) pages; the sequence with 4 pages on every device has length 65536.
All inputs are finite; a program needn't handle non-finite values.
Results may differ from a plain program's by a relative error of at most 0.007.
Values may be sent and summed in bfloat16 or wider, within the bound.
A program may use at most 64 MiB of HBM per device.

v0:
```python
import jax
import jax.numpy as jnp
from jax import lax
from jax.sharding import PartitionSpec as P

softmax_scale = 0.13528
floor_score = -1e30


def in_order(blocks, dim):
    blocks = jnp.moveaxis(blocks, 0, dim)
    lengths = blocks.shape
    return blocks.reshape(*lengths[:dim], lengths[dim] * lengths[dim + 1], *lengths[dim + 2 :])


def one_gather(arrays, axis, dims):
    vector = jnp.concatenate([a.reshape(-1) for a in arrays])
    lines, at, gathered = (lax.all_gather(vector, axis), 0, [])
    for a, dim in zip(arrays, dims):
        blocks = lines[:, at : at + a.size].reshape(-1, *a.shape)
        gathered.append(in_order(blocks, dim))
        at += a.size
    return tuple(gathered)


def from_everyone(array, axis):
    devices = lax.axis_size(axis)
    return lax.all_to_all(
        jnp.broadcast_to(array[None], (devices, *array.shape)), axis, 0, 0, tiled=True
    )


def gathered_copies(array, axis, dim):
    blocks = from_everyone(array, axis)
    return in_order(blocks, dim)


def side_by_side(arrays, axis, dim, along):
    ends, at = ([], 0)
    for a in arrays[:-1]:
        at += a.shape[along]
        ends.append(at)
    both = jnp.concatenate(arrays, axis=along)
    return tuple(jnp.split(gathered_copies(both, axis, dim), ends, axis=along))


def side_by_side_2(arrays, axis, dim, along):
    ends, at = ([], 0)
    for a in arrays[:-1]:
        at += a.shape[along]
        ends.append(at)
    both = jnp.concatenate(arrays, axis=along)
    return tuple(jnp.split(lax.all_gather(both, axis, axis=dim, tiled=True), ends, axis=along))


def split_up(array, dim, devices):
    lengths = array.shape
    blocks = array.reshape(*lengths[:dim], devices, lengths[dim] // devices, *lengths[dim + 1 :])
    return jnp.moveaxis(blocks, dim, 0)


def joined_exchange(array, axis, axes, splits, concats):
    sizes = [lax.axis_size(a) for a in axes]
    blocks = split_up(array, splits[0], sizes[0])
    blocks = jnp.moveaxis(split_up(blocks, splits[1] + 1, sizes[1]), 0, 1)
    inside = blocks.shape[2:]
    blocks = blocks.reshape(-1, *inside)
    blocks = lax.all_to_all(blocks, axis, split_axis=0, concat_axis=0, tiled=True)
    blocks = in_order(blocks.reshape(*sizes, *inside), concats[0] + 1)
    return in_order(blocks, concats[1])


def merge_sources(source_tops, source_totals, source_mixed):
    best_top = jnp.max(source_tops, axis=0)
    factor = jnp.exp(source_tops - best_top[None])
    total_sum = jnp.sum(factor * source_totals, axis=0)
    mixed_sum = jnp.sum(factor[..., None] * source_mixed, axis=0)
    return (mixed_sum / total_sum[..., None]).astype(jnp.bfloat16)


def on_device(q_latent, q_rope, cache_latent, cache_rope, page_table, lengths):
    slot_count, page_len, lat_width = cache_latent.shape
    seq_count = lax.axis_size("seq")
    group_count = lax.axis_size("head")
    seq_index = lax.axis_index("seq")
    head_index = lax.axis_index("head")
    tables, all_lengths = one_gather((page_table, lengths), "seq", (0, 0))
    row_width = tables.shape[1]
    head_lat, head_rot = side_by_side((q_latent, q_rope), "head", 1, 2)
    first_slot = (seq_index * group_count + head_index) * slot_count
    slot_ids = first_slot + jnp.arange(slot_count, dtype=jnp.int32)
    entry_ids = jnp.arange(seq_count * row_width, dtype=jnp.int32)
    matched = jnp.sum(
        jnp.where(tables.reshape(1, -1) == slot_ids[:, None], entry_ids[None, :] + 1, 0), axis=1
    )
    occupied = matched > 0
    entry_of = jnp.maximum(matched - 1, 0)
    slot_owner = entry_of // row_width
    page_number = entry_of % row_width
    seq_ids = jnp.arange(seq_count, dtype=jnp.int32)
    owner_hits = slot_owner[:, None] == seq_ids[None, :]
    owner_length = jnp.sum(jnp.where(owner_hits, all_lengths[None, :], 0), axis=1)
    position = page_number[:, None] * page_len + jnp.arange(page_len, dtype=jnp.int32)[None, :]
    token_live = occupied[:, None] & (position < owner_length[:, None])
    every_lat, every_rot = side_by_side_2((head_lat, head_rot), "seq", 0, 2)
    lat_query = every_lat[slot_owner]
    rot_query = every_rot[slot_owner]
    scores = jnp.einsum("bhd,btd->bht", lat_query, cache_latent, preferred_element_type=jnp.float32)
    scores = scores + jnp.einsum(
        "bhe,bet->bht", rot_query, cache_rope, preferred_element_type=jnp.float32
    )
    scores = jnp.where(token_live[:, None, :], scores * softmax_scale, floor_score)
    owner_pick = (slot_owner[None, :] == seq_ids[:, None]) & occupied[None, :]
    slot_top = jnp.max(scores, axis=2)
    all_top = jnp.max(jnp.where(owner_pick[:, :, None], slot_top[None], floor_score), axis=1)
    selector = owner_pick.astype(jnp.float32)
    slot_ref = jnp.einsum("sb,sh->bh", selector, all_top, precision=lax.Precision.HIGHEST)
    weight = jnp.where(token_live[:, None, :], jnp.exp(scores - slot_ref[:, :, None]), 0.0)
    all_total = jnp.einsum(
        "sb,bh->sh", selector, jnp.sum(weight, axis=2), precision=lax.Precision.HIGHEST
    )
    slot_mixed = jnp.einsum(
        "bht,btd->bhd",
        weight.astype(jnp.bfloat16),
        cache_latent,
        preferred_element_type=jnp.float32,
    )
    all_mixed = jnp.einsum("sb,bhd->shd", selector, slot_mixed, precision=lax.Precision.HIGHEST)
    source_tops, source_totals, source_mixed = (
        joined_exchange(all_top[None], ("seq", "head"), ("seq", "head"), (1, 2), (0, 0)),
        joined_exchange(all_total[None], ("seq", "head"), ("seq", "head"), (1, 2), (0, 0)),
        joined_exchange(all_mixed[None], ("seq", "head"), ("seq", "head"), (1, 2), (0, 0)),
    )
    return merge_sources(source_tops, source_totals, source_mixed)


def solution(mesh):
    placed = (
        P(("grp", "seq"), "head", None),
        P(("grp", "seq"), "head", None),
        P(("grp", "seq", "head"), None, None),
        P(("grp", "seq", "head"), None, None),
        P(("grp", "seq"), None),
        P(("grp", "seq")),
    )
    return jax.shard_map(
        on_device,
        mesh=mesh,
        in_specs=placed,
        out_specs=P(("grp", "seq"), "head", None),
        check_vma=False,
    )
```

profile of v0, /device:TPU:520, one launch (start us, length us, event | category | flops | bytes accessed | tf_op | source)
XLA Modules:
  0.0 287.5 jit_solution(11736804877574401514)
XLA Ops:
  6.5 0.0 copy-start
  6.6 0.0 all-gather.3.cloned.1.call-start
  6.6 0.8 maximum_bitcast_fusion
  7.4 25.4 %all_to_all.20 = bf16[8,1,16,576]{3,2,1,0:T(8,128)(2,1)S(1)} all-to-all(bf16[8,1,16,576]{3,2,1,0:T(8,128)(2,1)S(1)} %broadcast_in_dim.101), channel_id=1, replica_groups=mesh['grp'=2,'seq'=16,'head'=8] {'head'}, dimensions={0} | all-to-all | bytes 294912 | tf_op jit(solution)/shard_map/all_to_all | solution.py:28
  32.7 0.8 copy.25
  33.5 0.1 all-gather.3.cloned.1.call-update
  34.2 1.3 dynamic-slice
  36.2 0.8 add_dynamic-update-slice_fusion
  37.0 46.8 %all-reduce = s32[8208]{0:T(1024)S(1)} all-reduce(s32[8208]{0:T(1024)S(1)} %add_dynamic-update-slice_fusion), channel_id=2, replica_groups=mesh['grp'=2,'seq'=16,'head'=8] {'seq'}, use_global_device_ids=true, to_apply=%add | all-reduce | flops 8208 | bytes 65664
  83.8 0.1 reshape.283
  84.0 0.4 select_reduce_fusion
  84.4 0.1 copy.24
  84.5 0.1 slice_reduce_fusion
  84.6 0.1 select_reduce_fusion.2
  84.7 0.1 fusion.10
  84.8 0.0 all-gather.3.cloned.1.call-done
  84.9 1.0 split.11
  85.8 0.7 gather_fusion.1
  86.5 0.0 slice-start
  86.5 1.6 slice-done
  88.1 4.4 %gather_fusion = bf16[36,128,512]{1,2,0:T(8,128)(2,1)} fusion(bf16[16,128,512]{1,2,0:T(8,128)(2,1)S(1)} %slice-done, s32[1024]{0:T(1024)S(1)} %pad_clamp_fusion), kind=kCustom, calls=%fused_computation | custom fusion | bytes 9437328 | tf_op jit(solution)/shard_map/gather | solution.py:106
  92.5 0.0 copy-done
  92.5 0.5 fusion.22
  93.1 4.6 %fusion.21 = (f32[36,128]{1,0:T(8,128)S(1)}, f32[36,128,128]{1,2,0:T(8,128)S(1)}) fusion(f32[36,128,128]{1,2,0:T(8,128)S(1)} %fusion.22, bf16[36,128,512]{2,1,0:T(8,128)(2,1)} %param.8, bf16[36,128,512]{1,2,0:T(8,128)(2,1)} %gather_fusion, pred[36,128]{1,0:T(8,128)(4,1)S(1)} %fusion.10), kind=kOutput, calls=%fused_computation.45 | convolution fusion | flops 606334464 | bytes 14178816 | tf_op jit(solution)/shard_map/bhd,btd->bht/dot_general | solution.py:108
  97.6 0.1 select_reduce_fusion.1
  97.8 0.2 fusion.19
  98.0 1.0 fusion.2
  99.0 0.1 fusion.16
  99.1 0.7 reshape_transpose_transpose_reshape_transpose_reshape_broadcast_in_dim.11
  99.8 11.8 %all-to-all-start.3 = ((f32[128,1,1,16]{3,2,1,0:T(1,128)}), f32[128,1,1,16]{3,2,1,0:T(1,128)S(1)}, u32[]{:S(2)}, u32[]{:S(2)}) async-start(f32[128,1,1,16]{3,2,1,0:T(1,128)} %bitcast.18), calls=%async_computation.3 | async-start | bytes 131072 | tf_op jit(solution)/shard_map/all_to_all | solution.py:68
  111.6 6.6 %fusion.4 = f32[36,128,512]{2,1,0:T(8,128)} fusion(bf16[36,128,512]{2,1,0:T(8,128)(2,1)} %param.8, f32[36,128,128]{1,2,0:T(8,128)S(1)} %get-tuple-element.8, f32[36,128]{1,0:T(8,128)S(1)} %fusion.19, pred[36,128]{1,0:T(8,128)(4,1)S(1)} %fusion.10), kind=kOutput, calls=%fused_computation.10 | convolution fusion | flops 605749248 | bytes 16538112 | tf_op jit(solution)/shard_map/bht,btd->bhd/dot_general | solution.py:122
  118.2 0.7 reshape_transpose_transpose_reshape_transpose_reshape_broadcast_in_dim.9
  118.9 0.9 all-to-all-done.3
  119.8 15.5 %all-to-all-start.1 = ((f32[128,1,1,16]{3,2,1,0:T(1,128)}), f32[128,1,1,16]{3,2,1,0:T(1,128)S(1)}, u32[]{:S(2)}, u32[]{:S(2)}) async-start(f32[128,1,1,16]{3,2,1,0:T(1,128)} %bitcast.7), calls=%async_computation.1 | async-start | bytes 131072 | tf_op jit(solution)/shard_map/all_to_all | solution.py:68
  135.4 15.4 %fusion = f32[16,128,512]{2,0,1:T(8,128)S(1)} fusion(f32[36,128,512]{2,1,0:T(8,128)} %fusion.4, s32[36]{0:T(128)S(1)} %get-tuple-element.6, pred[36]{0:T(512)(128)(4,1)S(1)} %broadcast_compare_fusion), kind=kOutput, calls=%fused_computation.2 | convolution fusion | flops 452985984 | bytes 13631668 | tf_op jit(solution)/shard_map/sb,bhd->shd/dot_general | solution.py:128
  150.7 4.4 %copy.30 = f32[16,128,512]{2,1,0:T(8,128)} copy(f32[16,128,512]{2,0,1:T(8,128)S(1)} %fusion) | data formatting | bytes 8388608 | tf_op jit(solution)/shard_map/sb,bhd->shd/dot_general | solution.py:128
  155.1 0.0 all-to-all-done.1
  155.1 16.2 %all-to-all-start.2 = ((f32[128,1,1,16,512]{4,3,2,1,0:T(8,128)}), f32[128,1,1,16,512]{4,3,2,1,0:T(8,128)}, u32[]{:S(2)}, u32[]{:S(2)}) async-start(f32[128,1,1,16,512]{4,3,2,1,0:T(8,128)} %bitcast.50), calls=%async_computation.2 | async-start | bytes 8388608 | tf_op jit(solution)/shard_map/all_to_all | solution.py:68
  171.3 0.2 reduce_max.29
  171.6 105.9 %all-to-all-done.2 = f32[128,1,1,16,512]{4,3,2,1,0:T(8,128)} async-done(((f32[128,1,1,16,512]{4,3,2,1,0:T(8,128)}), f32[128,1,1,16,512]{4,3,2,1,0:T(8,128)}, u32[]{:S(2)}, u32[]{:S(2)}) %all-to-all-start.2) | async-done | bytes 4194336 | tf_op jit(solution)/shard_map/all_to_all | solution.py:68
  277.4 2.5 multiply_reduce_fusion
  280.0 0.7 fusion.9
  (13 shorter events, 0.2 us)
Async XLA Ops:
  6.5 86.0 %copy-start = (bf16[36,64,128]{2,1,0:T(8,128)(2,1)S(1)}, bf16[36,64,128]{2,1,0:T(8,128)(2,1)}, u32[]{:S(2)}) copy-start(bf16[36,64,128]{2,1,0:T(8,128)(2,1)} %param.9) | copy-start | bytes 1769476
  6.6 78.3 %all-gather.3.cloned.1.call-start = ((), (), s32[]{:S(2)}) async-start(), calls=%async_computation.4 | async-start | bytes 2506752 | tf_op jit(solution)/shard_map/all_gather | solution.py:53
  86.5 1.6 slice-start
  99.8 20.0 %all-to-all-start.3 = ((f32[128,1,1,16]{3,2,1,0:T(1,128)}), f32[128,1,1,16]{3,2,1,0:T(1,128)S(1)}, u32[]{:S(2)}, u32[]{:S(2)}) async-start(f32[128,1,1,16]{3,2,1,0:T(1,128)} %bitcast.18), calls=%async_computation.3 | async-start | bytes 131072 | tf_op jit(solution)/shard_map/all_to_all | solution.py:68
  119.8 35.3 %all-to-all-start.1 = ((f32[128,1,1,16]{3,2,1,0:T(1,128)}), f32[128,1,1,16]{3,2,1,0:T(1,128)S(1)}, u32[]{:S(2)}, u32[]{:S(2)}) async-start(f32[128,1,1,16]{3,2,1,0:T(1,128)} %bitcast.7), calls=%async_computation.1 | async-start | bytes 131072 | tf_op jit(solution)/shard_map/all_to_all | solution.py:68
  155.1 122.3 %all-to-all-start.2 = ((f32[128,1,1,16,512]{4,3,2,1,0:T(8,128)}), f32[128,1,1,16,512]{4,3,2,1,0:T(8,128)}, u32[]{:S(2)}, u32[]{:S(2)}) async-start(f32[128,1,1,16,512]{4,3,2,1,0:T(8,128)} %bitcast.50), calls=%async_computation.2 | async-start | bytes 8388608 | tf_op jit(solution)/shard_map/all_to_all | solution.py:68
Sparse Core Ops, SparseCore 0:
  33.7 44.7 all-gather.2
where the time goes:
time: 288 us; the launch traced here: 287 us
  waiting for transfers between devices  107 us (37%)
  blocking collectives  72.2 us (25%)
  starting transfers between devices  43.6 us (15%)
  matrix products  27.4 us (10%)
  local copies, waits for them, and re-layouts  15.8 us (5%)
  between operations  14.9 us (5%)
  other arithmetic  6.76 us (2%)
    all_to_all x3, waiting for transfers between devices, joined_exchange(): lax.all_to_all(blocks, axis, split_axis=0, concat_axis=0, tiled=True)  107 us
    unnamed x1, blocking collectives  46.8 us
    all_to_all x3, starting transfers between devices, joined_exchange(): lax.all_to_all(blocks, axis, split_axis=0, concat_axis=0, tiled=True)  43.6 us
    all_to_all x1, blocking collectives, from_everyone(): lax.all_to_all(jnp.broadcast_to(array[None], (devices, *array.shape)), ax...  25.4 us
    dot_general x1, matrix products, on_device(): jnp.einsum('sb,bhd->shd', selector, slot_mixed, precision=lax.Precision.H...  15.4 us
    dot_general x1, matrix products, on_device(): jnp.einsum('bht,btd->bhd', weight.astype(jnp.bfloat16), cache_latent, pre...  6.57 us
  transfers between devices with their start and end apart: 4, of which 2 were waited for; matrix products, arithmetic and copies ran while one was open for 11% of the time, Pallas kernels for 0%

commit v1 on v0

v1 whole, which is shorter than its diff:
```python
import functools

import jax
import jax.numpy as jnp
from jax import lax
from jax.experimental import pallas as pl
from jax.experimental.pallas import tpu as pltpu
from jax.sharding import PartitionSpec as P

softmax_scale = 0.13528
floor_score = -1e30
MESH = pl.DeviceIdType.MESH
MOST = 4
STAT = 128
bf16, f32 = jnp.bfloat16, jnp.float32


def kernel(
    n, heads, lat_w, rope_w, page, slots,
    q_hbm, t_hbm, lat_hbm, rope_hbm,
    out_ref,
    lat, rope, QB, TB, PB, RB, RR, MS, M2, FB, tvm, tsm,
    loc, a_send, a_recv, t_send, t_recv, g_send, g_recv, d_send, d_recv, td_send, td_recv,
    p_send, p_recv, r_send, r_recv, f_send, f_recv,
):
    half = n // 2
    sq = lax.axis_index("seq")
    x = lax.axis_index("head")
    y = sq // 2
    c = sq % 2
    a = x * (1 - c) + y * c
    b = y * (1 - c) + x * c

    def at(xx, yy, cc):
        return {"seq": 2 * yy + cc, "head": xx}

    def dev_a(i):
        return at(i * (1 - c) + x * c, y * (1 - c) + i * c, c)

    def dev_b(i):
        return at(x * (1 - c) + i * c, i * (1 - c) + y * c, c)

    sib = at(x, y, 1 - c)

    def rcopy(src, dst, ss, rs, dev):
        return pltpu.make_async_remote_copy(
            src_ref=src, dst_ref=dst, send_sem=ss, recv_sem=rs, device_id=dev, device_id_type=MESH
        )

    sends = []

    def send(src, dst, ss, rs, dev):
        cp = rcopy(src, dst, ss, rs, dev)
        cp.start()
        sends.append(cp)

    cq = pltpu.make_async_copy(q_hbm, QB.at[c, b, a], loc.at[0])
    ct = pltpu.make_async_copy(t_hbm, TB.at[c, y], loc.at[1])
    cl = pltpu.make_async_copy(lat_hbm, lat, loc.at[2])
    cr = pltpu.make_async_copy(rope_hbm, rope, loc.at[3])
    cq.start()
    ct.start()
    cl.start()
    cr.start()

    bar = pltpu.get_barrier_semaphore()
    for k in range(1, n):
        pl.semaphore_signal(bar, inc=1, device_id=dev_a((a + k) % n), device_id_type=MESH)
        pl.semaphore_signal(bar, inc=1, device_id=dev_b((b + k) % n), device_id_type=MESH)
    pl.semaphore_signal(bar, inc=1, device_id=sib, device_id_type=MESH)
    pl.semaphore_wait(bar, 2 * (n - 1) + 1)

    far = sorted(range(1, n), key=lambda k: -min(k, n - k))
    cq.wait()
    for k in far:
        send(QB.at[c, b, a], QB.at[c, b, a], a_send.at[k], a_recv.at[k], dev_a((a + k) % n))
    ct.wait()
    for k in far:
        send(TB.at[c, y], TB.at[c, y], t_send.at[k], t_recv.at[k], at(x, (y + k) % n, c))
    for k in far:
        rcopy(
            QB.at[c, b, (a - k) % n], QB.at[c, b, (a - k) % n], a_send.at[k], a_recv.at[k], sib
        ).wait_recv()

    def gpart(idx, h):
        return QB.at[c, idx, pl.ds(h * half, half)]

    right, left = dev_b((b + 1) % n), dev_b((b + n - 1) % n)
    nxt = (right, left)

    def origin(d, k):
        return (b + n - k) % n if d == 0 else (b + k) % n

    for h in range(2):
        for d in range(2):
            send(gpart(b, h), gpart(b, h), g_send.at[d, h], g_recv.at[d, h], nxt[d])
    send(QB.at[c, b], QB.at[c, b], d_send.at[2 * (n - 1)], d_recv.at[2 * (n - 1)], sib)

    for k in far:
        rcopy(
            TB.at[c, (y - k) % n], TB.at[c, (y - k) % n], t_send.at[k], t_recv.at[k], sib
        ).wait_recv()
    send(TB.at[c], TB.at[c], td_send.at[0], td_recv.at[0], sib)

    def ring_step(k):
        for j in range(2):
            for d in range(2):
                if k == half:
                    if j == 1:
                        continue
                    h, i = d, 2 * (half - 1)
                else:
                    h = j if d == 0 else 1 - j
                    i = 2 * (k - 1) + h
                part = gpart(origin(d, k), h)
                rcopy(part, part, g_send.at[d, i], g_recv.at[d, i], sib).wait_recv()
                if k < half - 1:
                    send(part, part, g_send.at[d, i + 2], g_recv.at[d, i + 2], nxt[d])
                elif k == half - 1 and h == d:
                    i2 = 2 * (half - 1)
                    send(part, part, g_send.at[d, i2], g_recv.at[d, i2], nxt[d])
                dd = d * (n - 1) + i
                send(part, part, d_send.at[dd], d_recv.at[dd], sib)

    b_sib = y * c + x * (1 - c)

    def d2d_wait(k):
        if k == 0:
            part = QB.at[1 - c, b_sib]
            i = 2 * (n - 1)
            rcopy(part, part, d_send.at[i], d_recv.at[i], sib).wait_recv()
            return
        for d in range(2):
            o = (b_sib + n - k) % n if d == 0 else (b_sib + k) % n
            for h in range(2):
                if k == half and h != d:
                    continue
                i = 2 * (k - 1) + h if k < half else 2 * (half - 1)
                part = QB.at[1 - c, o, pl.ds(h * half, half)]
                rcopy(
                    part, part, d_send.at[d * (n - 1) + i], d_recv.at[d * (n - 1) + i], sib
                ).wait_recv()

    def build_table():
        first = (sq * n + x) * slots * 256
        codes = TB[...].reshape(n * 16, 128)
        ok = (codes >= first) & (codes < first + slots * 256)
        key = jnp.where(ok, codes - first, -1).T
        row = lax.broadcasted_iota(jnp.int32, (8, 128), 0)
        lane = lax.broadcasted_iota(jnp.int32, (8, 128), 1)
        res = jnp.full((8, 128), -1, jnp.int32)
        for j in range(MOST):
            m = key
            size = key.shape[0]
            while size > 8:
                size //= 2
                m = jnp.maximum(m[:size], m[size:])
            for r in (4, 2, 1):
                m = jnp.maximum(m, pltpu.roll(m, r, 0))
            for bit in (1, 2, 4):
                part = jnp.where((lane & bit) > 0, pltpu.roll(m, bit, 1), pltpu.roll(m, 128 - bit, 1))
                m = jnp.maximum(m, part)
            res = jnp.where(row == j, m, res)
            key = jnp.where(key == jnp.concatenate([m] * 16, axis=0), -1, key)
        tvm[...] = res
        cp = pltpu.make_async_copy(tvm, tsm, loc.at[4])
        cp.start()
        cp.wait()

    def compute(par, yy):
        q = (QB[0, yy] if par == 0 else QB[1, :, yy]).reshape(n * heads, -1)
        ql, qr = q[:, :lat_w], q[:, lat_w : lat_w + rope_w]
        pages, parts = [], []
        lane = lax.broadcasted_iota(jnp.int32, (n * heads, page), 1)
        live = []
        for j in range(MOST):
            code = tsm[j, 8 * (par * n + yy)]
            slot = jnp.maximum(code, 0) // 256
            count = jnp.where(code < 0, 0, code % 256)
            pg = lat[slot]
            pages.append(pg)
            sc = lax.dot_general(ql, pg, (((1,), (1,)), ((), ())), preferred_element_type=f32)
            sc = sc + jnp.dot(qr, rope[slot], preferred_element_type=f32)
            ok = lane < count
            live.append(ok)
            parts.append(jnp.where(ok, sc * softmax_scale, floor_score))
        top = functools.reduce(jnp.maximum, parts)
        top = jnp.max(top, axis=1, keepdims=True).astype(bf16).astype(f32)
        ws = [jnp.where(o, jnp.exp(s - top), 0.0) for o, s in zip(live, parts)]
        total = jnp.sum(ws[0] + ws[1] + ws[2] + ws[3], axis=1, keepdims=True)
        w = jnp.concatenate([v.astype(bf16) for v in ws], axis=1)
        mixed = jnp.dot(w, jnp.concatenate(pages, axis=0), preferred_element_type=f32)
        full = jnp.concatenate([mixed.astype(bf16), stats(top, total)], axis=1)
        full = full.reshape(n, heads, lat_w + STAT)
        if par == 0:
            PB[0, yy] = full
        else:
            PB[1, :, yy] = full

        @pl.when(c == 1 - par)
        def _():
            part = PB.at[0, yy] if par == 0 else PB.at[1, :, yy]
            dst = RB.at[yy] if par == 0 else RB.at[:, yy]
            rcopy(part, dst, p_send.at[yy], p_recv.at[yy], sib).start()

    def stats(top, total):
        hi = total.astype(bf16)
        lo = (total - hi.astype(f32)).astype(bf16)
        lane = lax.broadcasted_iota(jnp.int32, (top.shape[0], STAT), 1)
        st = jnp.where(lane == 0, top, jnp.where(lane == 1, hi.astype(f32), lo.astype(f32)))
        return st.astype(bf16)

    def merge(values):
        tops, totals, mixes = [], [], []
        for v in values:
            st = v[:, lat_w:].astype(f32)
            tops.append(st[:, 0:1])
            totals.append(st[:, 1:2] + st[:, 2:3])
            mixes.append(v[:, :lat_w].astype(f32))
        top = functools.reduce(jnp.maximum, tops)
        fac = [jnp.exp(t - top) for t in tops]
        total = sum(f * t for f, t in zip(fac, totals))
        mixed = sum(f * m for f, m in zip(fac, mixes))
        return top, total, mixed

    def packed(top, total, mixed):
        return jnp.concatenate([mixed.astype(bf16), stats(top, total)], axis=1)

    ring_step(1)
    rcopy(TB.at[1 - c], TB.at[1 - c], td_send.at[0], td_recv.at[0], sib).wait_recv()
    build_table()
    cl.wait()
    cr.wait()
    d2d_wait(0)
    compute(0, y)
    for k in range(2, half + 1):
        ring_step(k)
        d2d_wait(k - 1)

        def pair(i, carry, k=k):
            compute(0, (y + n + (2 * i - 1) * (k - 1)) % n)
            return carry

        lax.fori_loop(0, 2, pair, 0)
    d2d_wait(half)
    compute(0, (y + half) % n)

    def odd(i, carry):
        compute(1, i)
        return carry

    lax.fori_loop(0, n, odd, 0)

    for i in range(n):
        rcopy(RB.at[i], RB.at[i], p_send.at[i], p_recv.at[i], sib).wait_recv()

    rows = half * heads

    def rslices(idx, h):
        s = pl.ds(h * half, half)
        return [PB[c, idx, s].reshape(rows, -1), RB[idx, s].reshape(rows, -1)]

    def ring_send(d, i, values):
        MS[d, i] = packed(*merge(values)).reshape(half, heads, -1)
        send(MS.at[d, i], RR.at[d, i], r_send.at[d, i], r_recv.at[d, i], nxt[d])

    def ring_recv(d, i):
        rcopy(RR.at[d, i], RR.at[d, i], r_send.at[d, i], r_recv.at[d, i], sib).wait_recv()
        return RR[d, i].reshape(rows, -1)

    def goal(d, k):
        return (b + k) % n if d == 0 else (b + n - k) % n

    for d in range(2):
        ring_send(d, 0, rslices(goal(d, half), d))
    for d in range(2):
        h = 1 - d
        ring_send(d, 1 + h, rslices(goal(d, half - 1), h))
    for d in range(2):
        ring_send(d, 1 + d, rslices(goal(d, half - 1), d) + [ring_recv(d, 0)])
    for k in range(3, half + 1):
        for j in range(2):
            for d in range(2):
                h = 1 - d if j == 0 else d
                i = 1 + 2 * (k - 2) + h
                ring_send(d, i, rslices(goal(d, half + 1 - k), h) + [ring_recv(d, i - 2)])
    for h in range(2):
        i = 1 + 2 * (half - 2) + h
        vals = rslices(b, h) + [ring_recv(0, i), ring_recv(1, i)]
        M2[pl.ds(h * half, half)] = packed(*merge(vals)).reshape(half, heads, -1)
    for k in far:
        o = (a + k) % n
        send(M2.at[o], FB.at[k], f_send.at[k], f_recv.at[k], dev_a(o))
    vals = [M2[a]]
    for k in far:
        rcopy(FB.at[k], FB.at[k], f_send.at[k], f_recv.at[k], sib).wait_recv()
        vals.append(FB[k])
    top, total, mixed = merge(vals)
    out_ref[...] = (mixed / total).astype(bf16)

    for cp in sends:
        cp.wait_send()
    for i in range(n):
        rcopy(RB.at[i], RB.at[i], p_send.at[i], p_recv.at[i], sib).wait_send()


def on_device(n, q_latent, q_rope, cache_latent, cache_rope, page_table, lengths):
    heads, lat_w = q_latent.shape[1:]
    rope_w = q_rope.shape[2]
    slots, page, _ = cache_latent.shape
    width = lat_w + STAT
    q = jnp.concatenate(
        [q_latent[0], q_rope[0], jnp.zeros((heads, width - lat_w - rope_w), bf16)], axis=1
    )
    maxp = page_table.shape[1]
    left = jnp.clip(lengths[0] - jnp.arange(maxp, dtype=jnp.int32) * page, 0, page)
    codes = jnp.where(page_table[0] >= 0, page_table[0] * 256 + left, -1).reshape(maxp // 128, 128)
    codes = jnp.concatenate([codes, jnp.full((8 - maxp // 128, 128), -1, jnp.int32)], axis=0)
    half = n // 2
    any_spec = pl.BlockSpec(memory_space=pl.ANY)
    dma = pltpu.SemaphoreType.DMA
    out = pl.pallas_call(
        functools.partial(kernel, n, heads, lat_w, rope_w, page, slots),
        out_shape=jax.ShapeDtypeStruct((heads, lat_w), bf16),
        in_specs=[any_spec] * 4,
        out_specs=pl.BlockSpec(memory_space=pltpu.VMEM),
        scratch_shapes=[
            pltpu.VMEM(cache_latent.shape, bf16),
            pltpu.VMEM(cache_rope.shape, bf16),
            pltpu.VMEM((2, n, n, heads, width), bf16),
            pltpu.VMEM((2, n, 8, 128), jnp.int32),
            pltpu.VMEM((2, n, n, heads, width), bf16),
            pltpu.VMEM((n, n, heads, width), bf16),
            pltpu.VMEM((2, n - 1, half, heads, width), bf16),
            pltpu.VMEM((2, n - 1, half, heads, width), bf16),
            pltpu.VMEM((n, heads, width), bf16),
            pltpu.VMEM((n, heads, width), bf16),
            pltpu.VMEM((8, 128), jnp.int32),
            pltpu.SMEM((8, 128), jnp.int32),
            dma((5,)),
            dma((n,)), dma((n,)), dma((n,)), dma((n,)),
            dma((2, n - 1)), dma((2, n - 1)),
            dma((2 * n - 1,)), dma((2 * n - 1,)),
            dma((1,)), dma((1,)),
            dma((n,)), dma((n,)),
            dma((2, n - 1)), dma((2, n - 1)),
            dma((n,)), dma((n,)),
        ],
        compiler_params=pltpu.CompilerParams(
            collective_id=0, has_side_effects=True, vmem_limit_bytes=48 * 1024 * 1024
        ),
    )(q, codes, cache_latent, cache_rope)
    return out[None]


def solution(mesh):
    n = mesh.shape["head"]
    assert mesh.shape["seq"] == 2 * n and n % 2 == 0
    placed = (
        P(("grp", "seq"), "head", None),
        P(("grp", "seq"), "head", None),
        P(("grp", "seq", "head"), None, None),
        P(("grp", "seq", "head"), None, None),
        P(("grp", "seq"), None),
        P(("grp", "seq")),
    )
    return jax.shard_map(
        functools.partial(on_device, n),
        mesh=mesh,
        in_specs=placed,
        out_specs=P(("grp", "seq"), "head", None),
        check_vma=False,
    )
```

time: 288 us -> 80 us (0.28)
  the two profiles are of different devices: /device:TPU:520 before, /device:TPU:514 now
where the time goes in v1:
time: 80 us; the launch traced here: 79.7 us
  Pallas kernels  72.8 us (91%)
  local copies, waits for them, and re-layouts  4.09 us (5%)
  other arithmetic  2.15 us (3%)
    pallas_call x1, Pallas kernels, on_device(): pl.pallas_call(functools.partial(kernel, n, heads, lat_w, rope_w, page, s...  72.8 us
    unnamed x5, local copies, waits for them, and re-layouts  4 us

profile of v1, /device:TPU:514, one launch (start us, length us, event | category | flops | bytes accessed | tf_op | source)
XLA Modules:
  0.0 79.7 jit_solution(3947299546171579751)
XLA Ops:
  0.7 0.7 compare_reduce_fusion
  1.4 0.1 pad.3.clone
  1.4 0.7 broadcast_multiply_fusion
  2.1 0.7 maximum_maximum_fusion.q_hbm
  2.9 0.0 copy-start
  2.9 2.3 %copy-done = bf16[36,128,512]{2,1,0:T(8,128)(2,1)S(1)} copy-done((bf16[36,128,512]{2,1,0:T(8,128)(2,1)S(1)}, bf16[36,128,512]{2,1,0:T(8,128)(2,1)}, u32[]{:S(2)}) %copy-start) | copy-done | bytes 4718616
  5.2 0.0 copy-start.1
  5.2 1.1 %copy-done.1 = bf16[36,64,128]{2,1,0:T(8,128)(2,1)S(1)} copy-done((bf16[36,64,128]{2,1,0:T(8,128)(2,1)S(1)}, bf16[36,64,128]{2,1,0:T(8,128)(2,1)}, u32[]{:S(2)}) %copy-start.1) | copy-done | bytes 589848
  6.3 72.8 %shard_map.64 = bf16[16,512]{1,0:T(8,128)(2,1)S(1)} custom-call(bf16[16,640]{1,0:T(8,128)(2,1)S(1)} %maximum_maximum_fusion.q_hbm, s32[8,128]{1,0:T(8,128)S(1)} %concatenate.7.t_hbm, bf16[36,128,512]{2,1,0:T(8,128)(2,1)S(1)} %copy-done, bf16[36,64,128]{2,1,0:T(8,128)(2,1)S(1)} %copy-done.1), custom_call_target="tpu_custom_call" | custom-call | tf_op jit(solution)/shard_map/pallas_call | solution.py:322
  79.1 0.6 copy.9
  (3 shorter events, 0.0 us)
Async XLA Ops:
  2.9 2.3 %copy-start = (bf16[36,128,512]{2,1,0:T(8,128)(2,1)S(1)}, bf16[36,128,512]{2,1,0:T(8,128)(2,1)}, u32[]{:S(2)}) copy-start(bf16[36,128,512]{2,1,0:T(8,128)(2,1)} %lat_hbm.1) | copy-start | bytes 14155780
  5.2 1.1 %copy-start.1 = (bf16[36,64,128]{2,1,0:T(8,128)(2,1)S(1)}, bf16[36,64,128]{2,1,0:T(8,128)(2,1)}, u32[]{:S(2)}) copy-start(bf16[36,64,128]{2,1,0:T(8,128)(2,1)} %rope_hbm.1) | copy-start | bytes 1769476

commit v2 on v1

v2 whole, which is shorter than its diff:
```python
import functools

import jax
import jax.numpy as jnp
from jax import lax
from jax.experimental import pallas as pl
from jax.experimental.pallas import tpu as pltpu
from jax.sharding import PartitionSpec as P

softmax_scale = 0.13528
floor_score = -1e30
MESH = pl.DeviceIdType.MESH
MOST = 4
STAT = 128
SUBS = 4
bf16, f32 = jnp.bfloat16, jnp.float32


def kernel(
    n, heads, lat_w, rope_w, page, slots,
    ql_hbm, qr_hbm, lat_hbm, rope_hbm, pt_hbm, len_ref,
    out_ref,
    lat, rope, QB, TB, SB, RB, LM, LT, LS, RR, MS, M2, FB, qrv, ptv, tvm, tsm,
    loc, a_send, a_recv, t_send, t_recv, g_send, g_recv, d_send, d_recv, td_send, td_recv,
    p_send, p_recv, r_send, r_recv, f_send, f_recv,
):
    half = n // 2
    per = n // SUBS
    lanes = lat_w // 128
    sq = lax.axis_index("seq")
    x = lax.axis_index("head")
    y = sq // 2
    c = sq % 2
    a = x * (1 - c) + y * c
    b = y * (1 - c) + x * c

    def at(xx, yy, cc):
        return {"seq": 2 * yy + cc, "head": xx}

    def dev_a(i):
        return at(i * (1 - c) + x * c, y * (1 - c) + i * c, c)

    def dev_b(i):
        return at(x * (1 - c) + i * c, i * (1 - c) + y * c, c)

    sib = at(x, y, 1 - c)

    def rcopy(src, dst, ss, rs, dev):
        return pltpu.make_async_remote_copy(
            src_ref=src, dst_ref=dst, send_sem=ss, recv_sem=rs, device_id=dev, device_id_type=MESH
        )

    sends = []

    def send(src, dst, ss, rs, dev):
        cp = rcopy(src, dst, ss, rs, dev)
        cp.start()
        sends.append(cp)

    bar = pltpu.get_barrier_semaphore()
    far = sorted(range(1, n), key=lambda k: -min(k, n - k))
    for k in far:
        pl.semaphore_signal(bar, inc=1, device_id=dev_a((a + k) % n), device_id_type=MESH)
        pl.semaphore_signal(bar, inc=1, device_id=dev_b((b + k) % n), device_id_type=MESH)
    pl.semaphore_signal(bar, inc=1, device_id=sib, device_id_type=MESH)

    own = QB.at[c, b, a]
    cq = pltpu.make_async_copy(ql_hbm.at[0], own.at[:, pl.ds(0, lat_w)], loc.at[0])
    cs = pltpu.make_async_copy(qr_hbm.at[0], qrv, loc.at[1])
    ct = pltpu.make_async_copy(pt_hbm, ptv, loc.at[2])
    cl = pltpu.make_async_copy(lat_hbm, lat, loc.at[3])
    cr = pltpu.make_async_copy(rope_hbm, rope, loc.at[4])
    cq.start()
    cs.start()
    ct.start()
    cl.start()
    cr.start()

    ct.wait()
    rows_t = []
    lane1 = lax.broadcasted_iota(jnp.int32, (1, 128), 1)
    entries = ptv.shape[1] // 128
    for r in range(entries):
        v = ptv[:, r * 128 : (r + 1) * 128]
        live = jnp.clip(len_ref[0] - (lane1 + r * 128) * page, 0, page)
        rows_t.append(jnp.where(v >= 0, v * 256 + live, -1))
    rows_t.append(jnp.full((8 - entries, 128), -1, jnp.int32))
    TB[c, y] = jnp.concatenate(rows_t, axis=0)
    cs.wait()
    QB[c, b, a, :, pl.ds(lat_w, STAT)] = jnp.concatenate(
        [qrv[...], jnp.zeros((heads, STAT - rope_w), bf16)], axis=1
    )
    cq.wait()

    pl.semaphore_wait(bar, 2 * (n - 1) + 1)

    for k in far:
        send(own, own, a_send.at[k], a_recv.at[k], dev_a((a + k) % n))
    for k in far:
        send(TB.at[c, y], TB.at[c, y], t_send.at[k], t_recv.at[k], at(x, (y + k) % n, c))
    for k in far:
        part = QB.at[c, b, (a + n - k) % n]
        rcopy(part, part, a_send.at[k], a_recv.at[k], sib).wait_recv()

    def gpart(idx, j):
        return QB.at[c, idx, pl.ds(j * per, per)]

    right, left = dev_b((b + 1) % n), dev_b((b + n - 1) % n)
    nxt = (right, left)
    order = (
        tuple(range(SUBS)),
        tuple(range(SUBS // 2, SUBS)) + tuple(range(SUBS // 2)),
    )
    own_i = 2 * (half * SUBS)

    for j in range(SUBS):
        for d in range(2):
            p = order[d][j]
            send(gpart(b, p), gpart(b, p), g_send.at[d, p], g_recv.at[d, p], nxt[d])
    send(QB.at[c, b], QB.at[c, b], d_send.at[own_i], d_recv.at[own_i], sib)

    for k in far:
        part = TB.at[c, (y + n - k) % n]
        rcopy(part, part, t_send.at[k], t_recv.at[k], sib).wait_recv()
    send(TB.at[c], TB.at[c], td_send.at[0], td_recv.at[0], sib)

    def ring_sub(k, j):
        if k == half and j >= SUBS // 2:
            return
        for d in range(2):
            p = order[d][j]
            o = (b + n - k) % n if d == 0 else (b + k) % n
            i = (k - 1) * SUBS + p
            part = gpart(o, p)
            rcopy(part, part, g_send.at[d, i], g_recv.at[d, i], sib).wait_recv()
            if k < half - 1 or (k == half - 1 and j < SUBS // 2):
                send(part, part, g_send.at[d, i + SUBS], g_recv.at[d, i + SUBS], nxt[d])
            dd = d * half * SUBS + i
            send(part, part, d_send.at[dd], d_recv.at[dd], sib)

    b_sib = y * c + x * (1 - c)

    def d2d_wait(k):
        if k == 0:
            part = QB.at[1 - c, b_sib]
            rcopy(part, part, d_send.at[own_i], d_recv.at[own_i], sib).wait_recv()
            return
        for j in range(SUBS if k < half else SUBS // 2):
            for d in range(2):
                p = order[d][j]
                o = (b_sib + n - k) % n if d == 0 else (b_sib + k) % n
                dd = d * half * SUBS + (k - 1) * SUBS + p
                part = QB.at[1 - c, o, pl.ds(p * per, per)]
                rcopy(part, part, d_send.at[dd], d_recv.at[dd], sib).wait_recv()

    def build_table():
        first = (sq * n + x) * slots * 256
        codes = TB[...].reshape(n * 16, 128)
        ok = (codes >= first) & (codes < first + slots * 256)
        key = jnp.where(ok, codes - first, -1).T
        row = lax.broadcasted_iota(jnp.int32, (8, 128), 0)
        lane = lax.broadcasted_iota(jnp.int32, (8, 128), 1)
        res = jnp.full((8, 128), -1, jnp.int32)
        for j in range(MOST):
            m = key
            size = key.shape[0]
            while size > 8:
                size //= 2
                m = jnp.maximum(m[:size], m[size:])
            for r in (4, 2, 1):
                m = jnp.maximum(m, pltpu.roll(m, r, 0))
            for bit in (1, 2, 4):
                other = jnp.where(
                    (lane & bit) > 0, pltpu.roll(m, bit, 1), pltpu.roll(m, 128 - bit, 1)
                )
                m = jnp.maximum(m, other)
            res = jnp.where(row == j, m, res)
            key = jnp.where(key == jnp.concatenate([m] * (n * 2), axis=0), -1, key)
        tvm[...] = res
        cp = pltpu.make_async_copy(tvm, tsm, loc.at[5])
        cp.start()
        cp.wait()

    def stats(top, total):
        hi = total.astype(bf16)
        lo = (total - hi.astype(f32)).astype(bf16)
        lane = lax.broadcasted_iota(jnp.int32, top.shape, 1)
        st = jnp.where(lane == 0, top, jnp.where(lane == 1, hi.astype(f32), lo.astype(f32)))
        return st.astype(bf16)

    def compute(par, yy):
        q = (QB[0, yy] if par == 0 else QB[1, :, yy]).reshape(n * heads, -1)
        ql, qr = q[:, :lat_w], q[:, lat_w : lat_w + rope_w]
        pages, ropes, counts = [], [], []
        for j in range(MOST):
            code = tsm[j, 8 * (par * n + yy)]
            slot = jnp.maximum(code, 0) // 256
            counts.append(jnp.where(code < 0, 0, code % 256))
            pages.append(lat[slot])
            ropes.append(rope[slot])
        keys = jnp.concatenate(pages, axis=0)
        sc = lax.dot_general(ql, keys, (((1,), (1,)), ((), ())), preferred_element_type=f32)
        sc = sc + jnp.dot(qr, jnp.concatenate(ropes, axis=1), preferred_element_type=f32)
        lane = lax.broadcasted_iota(jnp.int32, (n * heads, page), 1)
        live = [lane < v for v in counts]
        parts = [
            jnp.where(live[j], sc[:, j * page : (j + 1) * page] * softmax_scale, floor_score)
            for j in range(MOST)
        ]
        top = functools.reduce(jnp.maximum, parts)
        top = jnp.max(top, axis=1, keepdims=True).astype(bf16).astype(f32)
        ws = [jnp.where(o, jnp.exp(s - top), 0.0) for o, s in zip(live, parts)]
        total = jnp.sum(ws[0] + ws[1] + ws[2] + ws[3], axis=1, keepdims=True)
        w = jnp.concatenate([v.astype(bf16) for v in ws], axis=1)
        mixed = jnp.dot(w, keys, preferred_element_type=f32)
        top = jnp.broadcast_to(top, (n * heads, STAT))
        total = jnp.broadcast_to(total, (n * heads, STAT))
        shape = (n, heads, -1)

        @pl.when(c == par)
        def _():
            if par == 0:
                LM[yy] = mixed.reshape(shape)
                LT[yy] = top.reshape(shape)
                LS[yy] = total.reshape(shape)
            else:
                LM[:, yy] = mixed.reshape(shape)
                LT[:, yy] = top.reshape(shape)
                LS[:, yy] = total.reshape(shape)

        @pl.when(c == 1 - par)
        def _():
            full = jnp.concatenate([mixed.astype(bf16), stats(top, total)], axis=1)
            SB[yy] = full.reshape(shape)
            dst = RB.at[yy] if par == 0 else RB.at[:, yy]
            rcopy(SB.at[yy], dst, p_send.at[yy], p_recv.at[yy], sib).start()

    for j in range(SUBS):
        ring_sub(1, j)
    rcopy(TB.at[1 - c], TB.at[1 - c], td_send.at[0], td_recv.at[0], sib).wait_recv()
    build_table()
    cl.wait()
    cr.wait()
    d2d_wait(0)
    compute(0, y)
    for k in range(2, half + 1):
        for j in range(SUBS // 2):
            ring_sub(k, j)
        d2d_wait(k - 1)
        compute(0, (y + n - (k - 1)) % n)
        for j in range(SUBS // 2, SUBS):
            ring_sub(k, j)
        compute(0, (y + k - 1) % n)
    d2d_wait(half)
    compute(0, (y + half) % n)

    def odd(i, carry):
        compute(1, i)
        return carry

    lax.fori_loop(0, n, odd, 0)

    rows = half * heads
    er = lax.broadcasted_iota(jnp.int32, (STAT, 2 * STAT), 0)
    ec = lax.broadcasted_iota(jnp.int32, (STAT, 2 * STAT), 1)
    spread = jnp.where(
        ((er == 0) & (ec < STAT)) | ((er > 0) & (er < 3) & (ec >= STAT)), 1.0, 0.0
    ).astype(bf16)

    def opened(v):
        s = jnp.dot(v[:, lat_w:], spread, preferred_element_type=f32)
        tiles = [v[:, j * 128 : (j + 1) * 128].astype(f32) for j in range(lanes)]
        return tiles, s[:, :STAT], s[:, STAT:]

    def merge(states):
        top = functools.reduce(jnp.maximum, [s[1] for s in states])
        fac = [jnp.exp(s[1] - top) for s in states]
        total = sum(f * s[2] for f, s in zip(fac, states))
        tiles = [sum(f * s[0][j] for f, s in zip(fac, states)) for j in range(lanes)]
        return tiles, top, total

    def packed(state):
        tiles, top, total = state
        return jnp.concatenate([t.astype(bf16) for t in tiles] + [stats(top, total)], axis=1)

    def hs(h):
        return pl.ds(h * half, half)

    def local(idx, h):
        v = LM[idx, hs(h)].reshape(rows, lat_w)
        tiles = [v[:, j * 128 : (j + 1) * 128] for j in range(lanes)]
        return tiles, LT[idx, hs(h)].reshape(rows, STAT), LS[idx, hs(h)].reshape(rows, STAT)

    def both(idx, h):
        return merge([local(idx, h), opened(RB[idx, hs(h)].reshape(rows, -1))])

    def premerge(idx, h):
        tiles, top, total = both(idx, h)
        LM[idx, hs(h)] = jnp.concatenate(tiles, axis=1).reshape(half, heads, lat_w)
        LT[idx, hs(h)] = top.reshape(half, heads, STAT)
        LS[idx, hs(h)] = total.reshape(half, heads, STAT)

    def ring_send(d, i, state):
        MS[d, i] = packed(state).reshape(half, heads, -1)
        send(MS.at[d, i], RR.at[d, i], r_send.at[d, i], r_recv.at[d, i], nxt[d])

    def ring_recv(d, i):
        rcopy(RR.at[d, i], RR.at[d, i], r_send.at[d, i], r_recv.at[d, i], sib).wait_recv()
        return opened(RR[d, i].reshape(rows, -1))

    def goal(d, k):
        return (b + k) % n if d == 0 else (b + n - k) % n

    for i in range(n):
        rcopy(RB.at[i], RB.at[i], p_send.at[i], p_recv.at[i], sib).wait_recv()

    for d in range(2):
        ring_send(d, 0, both(goal(d, half), d))
    for d in range(2):
        ring_send(d, 2 - d, both(goal(d, half - 1), 1 - d))
    for d in range(2):
        premerge(goal(d, half - 1), d)

    def pre(i, carry):
        idx = (b + n - (half - 2) + i // 2) % n
        premerge(idx, i % 2)
        return carry

    lax.fori_loop(0, 2 * (2 * (half - 2) + 1), pre, 0)

    for d in range(2):
        ring_send(d, 1 + d, merge([local(goal(d, half - 1), d), ring_recv(d, 0)]))
    for k in range(3, half + 1):
        for j in range(2):
            for d in range(2):
                h = 1 - d if j == 0 else d
                i = 1 + 2 * (k - 2) + h
                ring_send(d, i, merge([local(goal(d, half + 1 - k), h), ring_recv(d, i - 2)]))
    for h in range(2):
        i = 1 + 2 * (half - 2) + h
        state = merge([local(b, h), ring_recv(0, i), ring_recv(1, i)])
        M2[hs(h)] = packed(state).reshape(half, heads, -1)
    for k in far:
        o = (a + k) % n
        send(M2.at[o], FB.at[k], f_send.at[k], f_recv.at[k], dev_a(o))
    states = [opened(M2[a])]
    for k in far:
        rcopy(FB.at[k], FB.at[k], f_send.at[k], f_recv.at[k], sib).wait_recv()
        states.append(opened(FB[k]))
    tiles, top, total = merge(states)
    out_ref[...] = jnp.concatenate([(t / total).astype(bf16) for t in tiles], axis=1)

    for cp in sends:
        cp.wait_send()
    for i in range(n):
        rcopy(SB.at[i], SB.at[i], p_send.at[i], p_recv.at[i], sib).wait_send()


def on_device(n, q_latent, q_rope, cache_latent, cache_rope, page_table, lengths):
    heads, lat_w = q_latent.shape[1:]
    rope_w = q_rope.shape[2]
    slots, page, _ = cache_latent.shape
    width = lat_w + STAT
    half = n // 2
    any_spec = pl.BlockSpec(memory_space=pl.ANY)
    dma = pltpu.SemaphoreType.DMA
    out = pl.pallas_call(
        functools.partial(kernel, n, heads, lat_w, rope_w, page, slots),
        out_shape=jax.ShapeDtypeStruct((heads, lat_w), bf16),
        in_specs=[any_spec] * 5 + [pl.BlockSpec(memory_space=pltpu.SMEM)],
        out_specs=pl.BlockSpec(memory_space=pltpu.VMEM),
        scratch_shapes=[
            pltpu.VMEM(cache_latent.shape, bf16),
            pltpu.VMEM(cache_rope.shape, bf16),
            pltpu.VMEM((2, n, n, heads, width), bf16),
            pltpu.VMEM((2, n, 8, 128), jnp.int32),
            pltpu.VMEM((n, n, heads, width), bf16),
            pltpu.VMEM((n, n, heads, width), bf16),
            pltpu.VMEM((n, n, heads, lat_w), f32),
            pltpu.VMEM((n, n, heads, STAT), f32),
            pltpu.VMEM((n, n, heads, STAT), f32),
            pltpu.VMEM((2, n - 1, half, heads, width), bf16),
            pltpu.VMEM((2, n - 1, half, heads, width), bf16),
            pltpu.VMEM((n, heads, width), bf16),
            pltpu.VMEM((n, heads, width), bf16),
            pltpu.VMEM((heads, rope_w), bf16),
            pltpu.VMEM(page_table.shape, jnp.int32),
            pltpu.VMEM((8, 128), jnp.int32),
            pltpu.SMEM((8, 128), jnp.int32),
            dma((6,)),
            dma((n,)), dma((n,)), dma((n,)), dma((n,)),
            dma((2, half * SUBS)), dma((2, half * SUBS)),
            dma((2 * half * SUBS + 1,)), dma((2 * half * SUBS + 1,)),
            dma((1,)), dma((1,)),
            dma((n,)), dma((n,)),
            dma((2, n - 1)), dma((2, n - 1)),
            dma((n,)), dma((n,)),
        ],
        compiler_params=pltpu.CompilerParams(
            collective_id=0, has_side_effects=True, vmem_limit_bytes=57 * 1024 * 1024
        ),
    )(q_latent, q_rope, cache_latent, cache_rope, page_table, lengths)
    return out[None]


def solution(mesh):
    n = mesh.shape["head"]
    assert mesh.shape["seq"] == 2 * n and n % 2 == 0
    placed = (
        P(("grp", "seq"), "head", None),
        P(("grp", "seq"), "head", None),
        P(("grp", "seq", "head"), None, None),
        P(("grp", "seq", "head"), None, None),
        P(("grp", "seq"), None),
        P(("grp", "seq")),
    )
    return jax.shard_map(
        functools.partial(on_device, n),
        mesh=mesh,
        in_specs=placed,
        out_specs=P(("grp", "seq"), "head", None),
        check_vma=False,
    )
```

time: 80 us -> 75.3 us (0.941)
  the two profiles are of different devices: /device:TPU:514 before, /device:TPU:528 now
where the time goes in v2:
time: 75.3 us; the launch traced here: 75 us
  Pallas kernels  73 us (97%)
  local copies, waits for them, and re-layouts  1.32 us (2%)
    pallas_call x1, Pallas kernels, on_device(): pl.pallas_call(functools.partial(kernel, n, heads, lat_w, rope_w, page, s...  73 us

profile of v2, /device:TPU:528, one launch (start us, length us, event | category | flops | bytes accessed | tf_op | source)
XLA Modules:
  0.0 75.0 jit_solution(12977411688942238982)
XLA Ops:
  0.7 73.0 %shard_map.64 = bf16[16,512]{1,0:T(8,128)(2,1)} custom-call(bf16[1,16,512]{2,1,0:T(8,128)(2,1)} %ql_hbm.1, bf16[1,16,64]{2,1,0:T(8,128)(2,1)} %qr_hbm.1, bf16[36,128,512]{2,1,0:T(8,128)(2,1)} %lat_hbm.1, bf16[36,64,128]{2,1,0:T(8,128)(2,1)} %rope_hbm.1, s32[1,512]{1,0:T(1,128)} %pt_hbm.1, s32[1]{0:T(128)S(6)} %copy.8.len_ref), custom_call_target="tpu_custom_call" | custom-call | tf_op jit(solution)/shard_map/pallas_call | solution.py:367
  73.7 1.3 %copy.9 = bf16[1,16,512]{2,1,0:T(8,128)(2,1)} copy(bf16[1,16,512]{2,1,0:T(8,128)(2,1)} %bitcast.1) | data formatting | bytes 32768

commit v3 on v2

--- a/solution.py
+++ b/solution.py
@@ -20,8 +20,8 @@
     n, heads, lat_w, rope_w, page, slots,
     ql_hbm, qr_hbm, lat_hbm, rope_hbm, pt_hbm, len_ref,
     out_ref,
-    lat, rope, QB, TB, SB, RB, LM, LT, LS, RR, MS, M2, FB, qrv, ptv, tvm, tsm,
-    loc, a_send, a_recv, t_send, t_recv, g_send, g_recv, d_send, d_recv, td_send, td_recv,
+    lat, rope, QB, TB, SB, RB, LM, LT, LS, RR, MS, M2, FB, qown, town, qrv, ptv, tvm, tsm,
+    loc, a_send, a_recv, t_send, t_recv, g_send, g_recv, d_send, d_recv, o_send, o_recv,
     p_send, p_recv, r_send, r_recv, f_send, f_recv,
 ):
     half = n // 2
@@ -59,20 +59,21 @@
 
     bar = pltpu.get_barrier_semaphore()
     far = sorted(range(1, n), key=lambda k: -min(k, n - k))
-    for k in far:
-        pl.semaphore_signal(bar, inc=1, device_id=dev_a((a + k) % n), device_id_type=MESH)
-        pl.semaphore_signal(bar, inc=1, device_id=dev_b((b + k) % n), device_id_type=MESH)
-    pl.semaphore_signal(bar, inc=1, device_id=sib, device_id_type=MESH)
-
-    own = QB.at[c, b, a]
-    cq = pltpu.make_async_copy(ql_hbm.at[0], own.at[:, pl.ds(0, lat_w)], loc.at[0])
+    partners = [at((x + k) % n, y, 1 - c) for k in far]
+    partners += [at(x, (y + k) % n, 1 - c) for k in far]
+    partners += [dev_a((a + k) % n) for k in far]
+    partners += [dev_b((b + 1) % n), dev_b((b + n - 1) % n), sib]
+    for dev in partners:
+        pl.semaphore_signal(bar, inc=1, device_id=dev, device_id_type=MESH)
+
+    cq = pltpu.make_async_copy(ql_hbm.at[0], qown.at[:, pl.ds(0, lat_w)], loc.at[0])
     cs = pltpu.make_async_copy(qr_hbm.at[0], qrv, loc.at[1])
     ct = pltpu.make_async_copy(pt_hbm, ptv, loc.at[2])
     cl = pltpu.make_async_copy(lat_hbm, lat, loc.at[3])
     cr = pltpu.make_async_copy(rope_hbm, rope, loc.at[4])
+    ct.start()
+    cs.start()
     cq.start()
-    cs.start()
-    ct.start()
     cl.start()
     cr.start()
 
@@ -85,73 +86,35 @@
         live = jnp.clip(len_ref[0] - (lane1 + r * 128) * page, 0, page)
         rows_t.append(jnp.where(v >= 0, v * 256 + live, -1))
     rows_t.append(jnp.full((8 - entries, 128), -1, jnp.int32))
-    TB[c, y] = jnp.concatenate(rows_t, axis=0)
+    town[...] = jnp.concatenate(rows_t, axis=0)
     cs.wait()
-    QB[c, b, a, :, pl.ds(lat_w, STAT)] = jnp.concatenate(
+    qown[:, pl.ds(lat_w, STAT)] = jnp.concatenate(
         [qrv[...], jnp.zeros((heads, STAT - rope_w), bf16)], axis=1
     )
     cq.wait()
 
-    pl.semaphore_wait(bar, 2 * (n - 1) + 1)
+    pl.semaphore_wait(bar, len(partners))
 
     for k in far:
-        send(own, own, a_send.at[k], a_recv.at[k], dev_a((a + k) % n))
+        dev = at((x + k * (1 - c)) % n, (y + k * c) % n, 1)
+        send(qown, QB.at[c, b, a], a_send.at[k], a_recv.at[c, k], dev)
     for k in far:
-        send(TB.at[c, y], TB.at[c, y], t_send.at[k], t_recv.at[k], at(x, (y + k) % n, c))
-    for k in far:
-        part = QB.at[c, b, (a + n - k) % n]
-        rcopy(part, part, a_send.at[k], a_recv.at[k], sib).wait_recv()
-
-    def gpart(idx, j):
-        return QB.at[c, idx, pl.ds(j * per, per)]
-
-    right, left = dev_b((b + 1) % n), dev_b((b + n - 1) % n)
-    nxt = (right, left)
+        send(town, TB.at[c, y], t_send.at[k], t_recv.at[c, k], at(x, (y + k) % n, 1))
+
+    def part_of(par, idx, p):
+        return QB.at[par, idx, pl.ds(p * per, per)]
+
     order = (
         tuple(range(SUBS)),
         tuple(range(SUBS // 2, SUBS)) + tuple(range(SUBS // 2)),
     )
-    own_i = 2 * (half * SUBS)
-
-    for j in range(SUBS):
-        for d in range(2):
-            p = order[d][j]
-            send(gpart(b, p), gpart(b, p), g_send.at[d, p], g_recv.at[d, p], nxt[d])
-    send(QB.at[c, b], QB.at[c, b], d_send.at[own_i], d_recv.at[own_i], sib)
-
-    for k in far:
-        part = TB.at[c, (y + n - k) % n]
-        rcopy(part, part, t_send.at[k], t_recv.at[k], sib).wait_recv()
-    send(TB.at[c], TB.at[c], td_send.at[0], td_recv.at[0], sib)
-
-    def ring_sub(k, j):
-        if k == half and j >= SUBS // 2:
-            return
-        for d in range(2):
-            p = order[d][j]
-            o = (b + n - k) % n if d == 0 else (b + k) % n
-            i = (k - 1) * SUBS + p
-            part = gpart(o, p)
-            rcopy(part, part, g_send.at[d, i], g_recv.at[d, i], sib).wait_recv()
-            if k < half - 1 or (k == half - 1 and j < SUBS // 2):
-                send(part, part, g_send.at[d, i + SUBS], g_recv.at[d, i + SUBS], nxt[d])
-            dd = d * half * SUBS + i
-            send(part, part, d_send.at[dd], d_recv.at[dd], sib)
-
-    b_sib = y * c + x * (1 - c)
-
-    def d2d_wait(k):
-        if k == 0:
-            part = QB.at[1 - c, b_sib]
-            rcopy(part, part, d_send.at[own_i], d_recv.at[own_i], sib).wait_recv()
-            return
-        for j in range(SUBS if k < half else SUBS // 2):
-            for d in range(2):
-                p = order[d][j]
-                o = (b_sib + n - k) % n if d == 0 else (b_sib + k) % n
-                dd = d * half * SUBS + (k - 1) * SUBS + p
-                part = QB.at[1 - c, o, pl.ds(p * per, per)]
-                rcopy(part, part, d_send.at[dd], d_recv.at[dd], sib).wait_recv()
+    mid = (y, x)
+
+    def origin(par, d, k):
+        return (mid[par] + n - k) % n if d == 0 else (mid[par] + k) % n
+
+    def subs_at(k):
+        return SUBS // 2 if k == half else SUBS
 
     def build_table():
         first = (sq * n + x) * slots * 256
@@ -188,7 +151,7 @@
         st = jnp.where(lane == 0, top, jnp.where(lane == 1, hi.astype(f32), lo.astype(f32)))
         return st.astype(bf16)
 
-    def compute(par, yy):
+    def compute(par, yy, own):
         q = (QB[0, yy] if par == 0 else QB[1, :, yy]).reshape(n * heads, -1)
         ql, qr = q[:, :lat_w], q[:, lat_w : lat_w + rope_w]
         pages, ropes, counts = [], [], []
@@ -217,48 +180,19 @@
         total = jnp.broadcast_to(total, (n * heads, STAT))
         shape = (n, heads, -1)
 
-        @pl.when(c == par)
-        def _():
-            if par == 0:
-                LM[yy] = mixed.reshape(shape)
-                LT[yy] = top.reshape(shape)
-                LS[yy] = total.reshape(shape)
-            else:
-                LM[:, yy] = mixed.reshape(shape)
-                LT[:, yy] = top.reshape(shape)
-                LS[:, yy] = total.reshape(shape)
-
-        @pl.when(c == 1 - par)
-        def _():
+        if own and par == 0:
+            LM[yy] = mixed.reshape(shape)
+            LT[yy] = top.reshape(shape)
+            LS[yy] = total.reshape(shape)
+        elif own:
+            LM[:, yy] = mixed.reshape(shape)
+            LT[:, yy] = top.reshape(shape)
+            LS[:, yy] = total.reshape(shape)
+        else:
             full = jnp.concatenate([mixed.astype(bf16), stats(top, total)], axis=1)
             SB[yy] = full.reshape(shape)
             dst = RB.at[yy] if par == 0 else RB.at[:, yy]
             rcopy(SB.at[yy], dst, p_send.at[yy], p_recv.at[yy], sib).start()
-
-    for j in range(SUBS):
-        ring_sub(1, j)
-    rcopy(TB.at[1 - c], TB.at[1 - c], td_send.at[0], td_recv.at[0], sib).wait_recv()
-    build_table()
-    cl.wait()
-    cr.wait()
-    d2d_wait(0)
-    compute(0, y)
-    for k in range(2, half + 1):
-        for j in range(SUBS // 2):
-            ring_sub(k, j)
-        d2d_wait(k - 1)
-        compute(0, (y + n - (k - 1)) % n)
-        for j in range(SUBS // 2, SUBS):
-            ring_sub(k, j)
-        compute(0, (y + k - 1) % n)
-    d2d_wait(half)
-    compute(0, (y + half) % n)
-
-    def odd(i, carry):
-        compute(1, i)
-        return carry
-
-    lax.fori_loop(0, n, odd, 0)
 
     rows = half * heads
     er = lax.broadcasted_iota(jnp.int32, (STAT, 2 * STAT), 0)
@@ -300,60 +234,190 @@
         LT[idx, hs(h)] = top.reshape(half, heads, STAT)
         LS[idx, hs(h)] = total.reshape(half, heads, STAT)
 
-    def ring_send(d, i, state):
-        MS[d, i] = packed(state).reshape(half, heads, -1)
-        send(MS.at[d, i], RR.at[d, i], r_send.at[d, i], r_recv.at[d, i], nxt[d])
-
-    def ring_recv(d, i):
-        rcopy(RR.at[d, i], RR.at[d, i], r_send.at[d, i], r_recv.at[d, i], sib).wait_recv()
-        return opened(RR[d, i].reshape(rows, -1))
-
     def goal(d, k):
         return (b + k) % n if d == 0 else (b + n - k) % n
 
-    for i in range(n):
-        rcopy(RB.at[i], RB.at[i], p_send.at[i], p_recv.at[i], sib).wait_recv()
-
-    for d in range(2):
-        ring_send(d, 0, both(goal(d, half), d))
-    for d in range(2):
-        ring_send(d, 2 - d, both(goal(d, half - 1), 1 - d))
-    for d in range(2):
-        premerge(goal(d, half - 1), d)
-
-    def pre(i, carry):
-        idx = (b + n - (half - 2) + i // 2) % n
-        premerge(idx, i % 2)
-        return carry
-
-    lax.fori_loop(0, 2 * (2 * (half - 2) + 1), pre, 0)
-
-    for d in range(2):
-        ring_send(d, 1 + d, merge([local(goal(d, half - 1), d), ring_recv(d, 0)]))
-    for k in range(3, half + 1):
-        for j in range(2):
-            for d in range(2):
-                h = 1 - d if j == 0 else d
-                i = 1 + 2 * (k - 2) + h
-                ring_send(d, i, merge([local(goal(d, half + 1 - k), h), ring_recv(d, i - 2)]))
-    for h in range(2):
-        i = 1 + 2 * (half - 2) + h
-        state = merge([local(b, h), ring_recv(0, i), ring_recv(1, i)])
-        M2[hs(h)] = packed(state).reshape(half, heads, -1)
-    for k in far:
-        o = (a + k) % n
-        send(M2.at[o], FB.at[k], f_send.at[k], f_recv.at[k], dev_a(o))
-    states = [opened(M2[a])]
-    for k in far:
-        rcopy(FB.at[k], FB.at[k], f_send.at[k], f_recv.at[k], sib).wait_recv()
-        states.append(opened(FB[k]))
-    tiles, top, total = merge(states)
-    out_ref[...] = jnp.concatenate([(t / total).astype(bf16) for t in tiles], axis=1)
+    nxt = (dev_b((b + 1) % n), dev_b((b + n - 1) % n))
+
+    def reduce(gaps):
+        out = []
+
+        def put(src, dst, ss, rs, dev):
+            cp = rcopy(src, dst, ss, rs, dev)
+            cp.start()
+            out.append(cp)
+
+        def ring_send(d, i, state):
+            MS[d, i] = packed(state).reshape(half, heads, -1)
+            put(MS.at[d, i], RR.at[d, i], r_send.at[d, i], r_recv.at[d, i], nxt[d])
+
+        def ring_recv(d, i):
+            rcopy(RR.at[d, i], RR.at[d, i], r_send.at[d, i], r_recv.at[d, i], sib).wait_recv()
+            return opened(RR[d, i].reshape(rows, -1))
+
+        def pre(k):
+            for d in range(2 if k else 1):
+                for h in range(2):
+                    premerge(goal(d, k), h)
+
+        for i in range(n):
+            rcopy(RB.at[i], RB.at[i], p_send.at[i], p_recv.at[i], sib).wait_recv()
+        for d in range(2):
+            ring_send(d, 0, both(goal(d, half), d))
+        for d in range(2):
+            ring_send(d, 2 - d, both(goal(d, half - 1), 1 - d))
+        for d in range(2):
+            premerge(goal(d, half - 1), d)
+        gaps[0]()
+        for d in range(2):
+            ring_send(d, 1 + d, merge([local(goal(d, half - 1), d), ring_recv(d, 0)]))
+        for k in range(3, half + 1):
+            pre(half + 1 - k)
+            gaps[k - 2]()
+            for j in range(2):
+                for d in range(2):
+                    h = 1 - d if j == 0 else d
+                    i = 1 + 2 * (k - 2) + h
+                    ring_send(d, i, merge([local(goal(d, half + 1 - k), h), ring_recv(d, i - 2)]))
+        pre(0)
+        gaps[half - 1]()
+        for h in range(2):
+            i = 1 + 2 * (half - 2) + h
+            state = merge([local(b, h), ring_recv(0, i), ring_recv(1, i)])
+            M2[hs(h)] = packed(state).reshape(half, heads, -1)
+        for k in far:
+            o = (a + k) % n
+            put(M2.at[o], FB.at[k], f_send.at[k], f_recv.at[k], dev_a(o))
+        states = [opened(M2[a])]
+        for k in far:
+            rcopy(FB.at[k], FB.at[k], f_send.at[k], f_recv.at[k], sib).wait_recv()
+            states.append(opened(FB[k]))
+        tiles, top, total = merge(states)
+        out_ref[...] = jnp.concatenate([(t / total).astype(bf16) for t in tiles], axis=1)
+        for i in range(n):
+            rcopy(SB.at[i], SB.at[i], p_send.at[i], p_recv.at[i], sib).wait_send()
+        for cp in out:
+            cp.wait_send()
+
+    def nothing():
+        return
+
+    @pl.when(c == 1)
+    def _():
+        out = []
+
+        def put(src, dst, ss, rs, dev):
+            cp = rcopy(src, dst, ss, rs, dev)
+            cp.start()
+            out.append(cp)
+
+        neighbour = (
+            (at(x, (y + 1) % n, 1), at(x, (y + n - 1) % n, 1)),
+            (at((x + 1) % n, y, 1), at((x + n - 1) % n, y, 1)),
+        )
+        QB[1, x, y] = qown[...]
+        TB[1, y] = town[...]
+        for par in (1, 0):
+            for k in far + ([0] if par == 0 else []):
+                src = (x + n - k) % n if par == 0 else (y + n - k) % n
+                part = QB.at[par, mid[par], src]
+                rcopy(part, part, a_send.at[k], a_recv.at[par, k], sib).wait_recv()
+            for j in range(SUBS):
+                for d in range(2):
+                    p = order[d][j]
+                    part = part_of(par, mid[par], p)
+                    put(part, part, g_send.at[par, d, p], g_recv.at[par, d, p], neighbour[par][d])
+            part = QB.at[par, mid[par]]
+            put(part, part, o_send.at[par], o_recv.at[par], sib)
+        for par in (1, 0):
+            for k in far + ([0] if par == 0 else []):
+                part = TB.at[par, (y + n - k) % n]
+                rcopy(part, part, t_send.at[k], t_recv.at[par, k], sib).wait_recv()
+        put(TB, TB, o_send.at[2], o_recv.at[2], sib)
+        build_table()
+        cl.wait()
+        cr.wait()
+
+        def ring_sub(k, j):
+            for par in (1, 0):
+                for d in range(2):
+                    p = order[d][j]
+                    i = (k - 1) * SUBS + p
+                    part = part_of(par, origin(par, d, k), p)
+                    rcopy(part, part, g_send.at[par, d, i], g_recv.at[par, d, i], sib).wait_recv()
+                    if k < half - 1 or (k == half - 1 and j < SUBS // 2):
+                        i2 = i + SUBS
+                        ss, rs = g_send.at[par, d, i2], g_recv.at[par, d, i2]
+                        put(part, part, ss, rs, neighbour[par][d])
+                    put(part, part, d_send.at[par, d, i], d_recv.at[par, d, i], sib)
+
+        compute(0, y, False)
+        rest = [(y + half) % n]
+        for k in range(half - 1, 0, -1):
+            rest += [(y + n - k) % n, (y + k) % n]
+        for k in range(1, half + 1):
+            for j in range(subs_at(k)):
+                ring_sub(k, j)
+            if k < half:
+                compute(0, rest.pop(), False)
+        while rest:
+            compute(0, rest.pop(), False)
+
+        def odd(i, carry):
+            compute(1, i, True)
+            return carry
+
+        lax.fori_loop(0, n, odd, 0)
+        reduce([nothing] * half)
+        for cp in out:
+            cp.wait_send()
+
+    @pl.when(c == 0)
+    def _():
+        put_a = rcopy(qown, QB.at[0, y, x], a_send.at[0], a_recv.at[0, 0], sib)
+        put_t = rcopy(town, TB.at[0, y], t_send.at[0], t_recv.at[0, 0], sib)
+        put_a.start()
+        put_t.start()
+
+        def arrived(par, k):
+            if k == 0:
+                part = QB.at[par, mid[par]]
+                rcopy(part, part, o_send.at[par], o_recv.at[par], sib).wait_recv()
+                return
+            for j in range(subs_at(k)):
+                for d in range(2):
+                    p = order[d][j]
+                    i = (k - 1) * SUBS + p
+                    part = part_of(par, origin(par, d, k), p)
+                    rcopy(part, part, d_send.at[par, d, i], d_recv.at[par, d, i], sib).wait_recv()
+
+        rcopy(TB, TB, o_send.at[2], o_recv.at[2], sib).wait_recv()
+        build_table()
+        cl.wait()
+        cr.wait()
+        arrived(0, 0)
+        compute(0, y, True)
+        for k in range(1, half + 1):
+            arrived(0, k)
+            compute(0, (y + n - k) % n, True)
+            if k < half:
+                compute(0, (y + k) % n, True)
+        for k in range(half + 1):
+            arrived(1, k)
+
+        def odds(first, last):
+            def body(i, carry):
+                compute(1, i, False)
+                return carry
+
+            return lambda: lax.fori_loop(first, last, body, 0) and None
+
+        reduce([odds(0, 3 * n // 4), odds(3 * n // 4, n)] + [nothing] * (half - 2))
+        put_a.wait_send()
+        put_t.wait_send()
 
     for cp in sends:
         cp.wait_send()
-    for i in range(n):
-        rcopy(SB.at[i], SB.at[i], p_send.at[i], p_recv.at[i], sib).wait_send()
 
 
 def on_device(n, q_latent, q_rope, cache_latent, cache_rope, page_table, lengths):
@@ -383,15 +447,17 @@
             pltpu.VMEM((2, n - 1, half, heads, width), bf16),
             pltpu.VMEM((n, heads, width), bf16),
             pltpu.VMEM((n, heads, width), bf16),
+            pltpu.VMEM((heads, width), bf16),
+            pltpu.VMEM((8, 128), jnp.int32),
             pltpu.VMEM((heads, rope_w), bf16),
             pltpu.VMEM(page_table.shape, jnp.int32),
             pltpu.VMEM((8, 128), jnp.int32),
             pltpu.SMEM((8, 128), jnp.int32),
             dma((6,)),
-            dma((n,)), dma((n,)), dma((n,)), dma((n,)),
-            dma((2, half * SUBS)), dma((2, half * SUBS)),
-            dma((2 * half * SUBS + 1,)), dma((2 * half * SUBS + 1,)),
-            dma((1,)), dma((1,)),
+            dma((n,)), dma((2, n)), dma((n,)), dma((2, n)),
+            dma((2, 2, half * SUBS)), dma((2, 2, half * SUBS)),
+            dma((2, 2, half * SUBS)), dma((2, 2, half * SUBS)),
+            dma((3,)), dma((3,)),
             dma((n,)), dma((n,)),
             dma((2, n - 1)), dma((2, n - 1)),
             dma((n,)), dma((n,)),

time: 75.3 us -> 75.9 us (level)
  the two profiles are of different devices: /device:TPU:528 before, /device:TPU:513 now
where the time goes in v3:
time: 75.9 us; the launch traced here: 75.7 us
  Pallas kernels  73.7 us (97%)
  local copies, waits for them, and re-layouts  1.32 us (2%)
    pallas_call x1, Pallas kernels, on_device(): pl.pallas_call(functools.partial(kernel, n, heads, lat_w, rope_w, page, s...  73.7 us

profile of v3, /device:TPU:513, one launch (start us, length us, event | category | flops | bytes accessed | tf_op | source)
XLA Modules:
  0.0 75.7 jit_solution(16609533809064098170)
XLA Ops:
  0.7 73.7 %shard_map.64 = bf16[16,512]{1,0:T(8,128)(2,1)} custom-call(bf16[1,16,512]{2,1,0:T(8,128)(2,1)} %ql_hbm.1, bf16[1,16,64]{2,1,0:T(8,128)(2,1)} %qr_hbm.1, bf16[36,128,512]{2,1,0:T(8,128)(2,1)} %lat_hbm.1, bf16[36,64,128]{2,1,0:T(8,128)(2,1)} %rope_hbm.1, s32[1,512]{1,0:T(1,128)} %pt_hbm.1, s32[1]{0:T(128)S(6)} %copy.8.len_ref), custom_call_target="tpu_custom_call" | custom-call | tf_op jit(solution)/shard_map/pallas_call | solution.py:431
  74.3 1.3 %copy.9 = bf16[1,16,512]{2,1,0:T(8,128)(2,1)} copy(bf16[1,16,512]{2,1,0:T(8,128)(2,1)} %bitcast.1) | data formatting | bytes 32768

commit v4 on v3

--- a/solution.py
+++ b/solution.py
@@ -37,12 +37,6 @@
     def at(xx, yy, cc):
         return {"seq": 2 * yy + cc, "head": xx}
 
-    def dev_a(i):
-        return at(i * (1 - c) + x * c, y * (1 - c) + i * c, c)
-
-    def dev_b(i):
-        return at(x * (1 - c) + i * c, i * (1 - c) + y * c, c)
-
     sib = at(x, y, 1 - c)
 
     def rcopy(src, dst, ss, rs, dev):
@@ -61,10 +55,16 @@
     far = sorted(range(1, n), key=lambda k: -min(k, n - k))
     partners = [at((x + k) % n, y, 1 - c) for k in far]
     partners += [at(x, (y + k) % n, 1 - c) for k in far]
-    partners += [dev_a((a + k) % n) for k in far]
-    partners += [dev_b((b + 1) % n), dev_b((b + n - 1) % n), sib]
+    partners += [sib]
+    ring = [at(x, (y + k) % n, 1) for k in far]
+    ring += [at((x + 1) % n, y, 1), at((x + n - 1) % n, y, 1)]
     for dev in partners:
         pl.semaphore_signal(bar, inc=1, device_id=dev, device_id_type=MESH)
+
+    @pl.when(c == 1)
+    def _():
+        for dev in ring:
+            pl.semaphore_signal(bar, inc=1, device_id=dev, device_id_type=MESH)
 
     cq = pltpu.make_async_copy(ql_hbm.at[0], qown.at[:, pl.ds(0, lat_w)], loc.at[0])
     cs = pltpu.make_async_copy(qr_hbm.at[0], qrv, loc.at[1])
@@ -93,7 +93,7 @@
     )
     cq.wait()
 
-    pl.semaphore_wait(bar, len(partners))
+    pl.semaphore_wait(bar, len(partners) + len(ring) * c)
 
     for k in far:
         dev = at((x + k * (1 - c)) % n, (y + k * c) % n, 1)
@@ -121,28 +121,24 @@
         codes = TB[...].reshape(n * 16, 128)
         ok = (codes >= first) & (codes < first + slots * 256)
         key = jnp.where(ok, codes - first, -1).T
+        keys = [key] + [pltpu.roll(key, 128 - r, 1) for r in range(1, entries)]
         row = lax.broadcasted_iota(jnp.int32, (8, 128), 0)
-        lane = lax.broadcasted_iota(jnp.int32, (8, 128), 1)
         res = jnp.full((8, 128), -1, jnp.int32)
         for j in range(MOST):
-            m = key
-            size = key.shape[0]
+            m = functools.reduce(jnp.maximum, keys)
+            size = m.shape[0]
             while size > 8:
                 size //= 2
                 m = jnp.maximum(m[:size], m[size:])
             for r in (4, 2, 1):
                 m = jnp.maximum(m, pltpu.roll(m, r, 0))
-            for bit in (1, 2, 4):
-                other = jnp.where(
-                    (lane & bit) > 0, pltpu.roll(m, bit, 1), pltpu.roll(m, 128 - bit, 1)
-                )
-                m = jnp.maximum(m, other)
             res = jnp.where(row == j, m, res)
-            key = jnp.where(key == jnp.concatenate([m] * (n * 2), axis=0), -1, key)
+            full = jnp.concatenate([m] * (n * 2), axis=0)
+            keys = [jnp.where(v == full, -1, v) for v in keys]
         tvm[...] = res
         cp = pltpu.make_async_copy(tvm, tsm, loc.at[5])
         cp.start()
-        cp.wait()
+        return cp
 
     def stats(top, total):
         hi = total.astype(bf16)
@@ -180,21 +176,20 @@
         total = jnp.broadcast_to(total, (n * heads, STAT))
         shape = (n, heads, -1)
 
-        if own and par == 0:
-            LM[yy] = mixed.reshape(shape)
-            LT[yy] = top.reshape(shape)
-            LS[yy] = total.reshape(shape)
-        elif own:
-            LM[:, yy] = mixed.reshape(shape)
-            LT[:, yy] = top.reshape(shape)
-            LS[:, yy] = total.reshape(shape)
+        if own:
+            for ref, v in ((LM, mixed), (LT, top), (LS, total)):
+                if par == 0:
+                    ref[0, yy] = v.reshape(shape)
+                else:
+                    ref[1, :, yy] = v.reshape(shape)
         else:
             full = jnp.concatenate([mixed.astype(bf16), stats(top, total)], axis=1)
-            SB[yy] = full.reshape(shape)
-            dst = RB.at[yy] if par == 0 else RB.at[:, yy]
-            rcopy(SB.at[yy], dst, p_send.at[yy], p_recv.at[yy], sib).start()
-
-    rows = half * heads
+            SB[par, yy] = full.reshape(shape)
+            dst = RB.at[0, yy] if par == 0 else RB.at[1, :, yy]
+            i = par * n + yy
+            rcopy(SB.at[par, yy], dst, p_send.at[i], p_recv.at[i], sib).start()
+
+    rows = per * heads
     er = lax.broadcasted_iota(jnp.int32, (STAT, 2 * STAT), 0)
     ec = lax.broadcasted_iota(jnp.int32, (STAT, 2 * STAT), 1)
     spread = jnp.where(
@@ -217,90 +212,26 @@
         tiles, top, total = state
         return jnp.concatenate([t.astype(bf16) for t in tiles] + [stats(top, total)], axis=1)
 
-    def hs(h):
-        return pl.ds(h * half, half)
-
-    def local(idx, h):
-        v = LM[idx, hs(h)].reshape(rows, lat_w)
+    def ps(p):
+        return pl.ds(p * per, per)
+
+    def both(par, idx, p):
+        v = LM[par, idx, ps(p)].reshape(rows, lat_w)
         tiles = [v[:, j * 128 : (j + 1) * 128] for j in range(lanes)]
-        return tiles, LT[idx, hs(h)].reshape(rows, STAT), LS[idx, hs(h)].reshape(rows, STAT)
-
-    def both(idx, h):
-        return merge([local(idx, h), opened(RB[idx, hs(h)].reshape(rows, -1))])
-
-    def premerge(idx, h):
-        tiles, top, total = both(idx, h)
-        LM[idx, hs(h)] = jnp.concatenate(tiles, axis=1).reshape(half, heads, lat_w)
-        LT[idx, hs(h)] = top.reshape(half, heads, STAT)
-        LS[idx, hs(h)] = total.reshape(half, heads, STAT)
-
-    def goal(d, k):
-        return (b + k) % n if d == 0 else (b + n - k) % n
-
-    nxt = (dev_b((b + 1) % n), dev_b((b + n - 1) % n))
-
-    def reduce(gaps):
-        out = []
-
-        def put(src, dst, ss, rs, dev):
-            cp = rcopy(src, dst, ss, rs, dev)
-            cp.start()
-            out.append(cp)
-
-        def ring_send(d, i, state):
-            MS[d, i] = packed(state).reshape(half, heads, -1)
-            put(MS.at[d, i], RR.at[d, i], r_send.at[d, i], r_recv.at[d, i], nxt[d])
-
-        def ring_recv(d, i):
-            rcopy(RR.at[d, i], RR.at[d, i], r_send.at[d, i], r_recv.at[d, i], sib).wait_recv()
-            return opened(RR[d, i].reshape(rows, -1))
-
-        def pre(k):
-            for d in range(2 if k else 1):
-                for h in range(2):
-                    premerge(goal(d, k), h)
-
-        for i in range(n):
-            rcopy(RB.at[i], RB.at[i], p_send.at[i], p_recv.at[i], sib).wait_recv()
-        for d in range(2):
-            ring_send(d, 0, both(goal(d, half), d))
-        for d in range(2):
-            ring_send(d, 2 - d, both(goal(d, half - 1), 1 - d))
-        for d in range(2):
-            premerge(goal(d, half - 1), d)
-        gaps[0]()
-        for d in range(2):
-            ring_send(d, 1 + d, merge([local(goal(d, half - 1), d), ring_recv(d, 0)]))
-        for k in range(3, half + 1):
-            pre(half + 1 - k)
-            gaps[k - 2]()
-            for j in range(2):
-                for d in range(2):
-                    h = 1 - d if j == 0 else d
-                    i = 1 + 2 * (k - 2) + h
-                    ring_send(d, i, merge([local(goal(d, half + 1 - k), h), ring_recv(d, i - 2)]))
-        pre(0)
-        gaps[half - 1]()
-        for h in range(2):
-            i = 1 + 2 * (half - 2) + h
-            state = merge([local(b, h), ring_recv(0, i), ring_recv(1, i)])
-            M2[hs(h)] = packed(state).reshape(half, heads, -1)
-        for k in far:
-            o = (a + k) % n
-            put(M2.at[o], FB.at[k], f_send.at[k], f_recv.at[k], dev_a(o))
-        states = [opened(M2[a])]
-        for k in far:
-            rcopy(FB.at[k], FB.at[k], f_send.at[k], f_recv.at[k], sib).wait_recv()
-            states.append(opened(FB[k]))
-        tiles, top, total = merge(states)
+        top = LT[par, idx, ps(p)].reshape(rows, STAT)
+        total = LS[par, idx, ps(p)].reshape(rows, STAT)
+        return [(tiles, top, total), opened(RB[par, idx, ps(p)].reshape(rows, -1))]
+
+    def goal(par, d, k):
+        return (mid[par] + k) % n if d == 0 else (mid[par] + n - k) % n
+
+    def halves(d):
+        lo, hi = tuple(range(SUBS // 2)), tuple(range(SUBS // 2, SUBS))
+        return (hi, lo) if d == 0 else (lo, hi)
+
+    def owned(values):
+        tiles, top, total = merge(values)
         out_ref[...] = jnp.concatenate([(t / total).astype(bf16) for t in tiles], axis=1)
-        for i in range(n):
-            rcopy(SB.at[i], SB.at[i], p_send.at[i], p_recv.at[i], sib).wait_send()
-        for cp in out:
-            cp.wait_send()
-
-    def nothing():
-        return
 
     @pl.when(c == 1)
     def _():
@@ -329,15 +260,6 @@
                     put(part, part, g_send.at[par, d, p], g_recv.at[par, d, p], neighbour[par][d])
             part = QB.at[par, mid[par]]
             put(part, part, o_send.at[par], o_recv.at[par], sib)
-        for par in (1, 0):
-            for k in far + ([0] if par == 0 else []):
-                part = TB.at[par, (y + n - k) % n]
-                rcopy(part, part, t_send.at[k], t_recv.at[par, k], sib).wait_recv()
-        put(TB, TB, o_send.at[2], o_recv.at[2], sib)
-        build_table()
-        cl.wait()
-        cr.wait()
-
         def ring_sub(k, j):
             for par in (1, 0):
                 for d in range(2):
@@ -351,24 +273,113 @@
                         put(part, part, ss, rs, neighbour[par][d])
                     put(part, part, d_send.at[par, d, i], d_recv.at[par, d, i], sib)
 
-        compute(0, y, False)
-        rest = [(y + half) % n]
-        for k in range(half - 1, 0, -1):
-            rest += [(y + n - k) % n, (y + k) % n]
-        for k in range(1, half + 1):
+        def ring_all(k):
             for j in range(subs_at(k)):
                 ring_sub(k, j)
-            if k < half:
-                compute(0, rest.pop(), False)
-        while rest:
-            compute(0, rest.pop(), False)
-
-        def odd(i, carry):
-            compute(1, i, True)
+
+        ring_all(1)
+        for par in (1, 0):
+            for k in far + ([0] if par == 0 else []):
+                part = TB.at[par, (y + n - k) % n]
+                rcopy(part, part, t_send.at[k], t_recv.at[par, k], sib).wait_recv()
+        put(TB, TB, o_send.at[2], o_recv.at[2], sib)
+        built = build_table()
+        cl.wait()
+        cr.wait()
+        ring_all(2)
+        built.wait()
+        compute(0, y, True)
+        ring_all(3)
+        compute(0, (y + 1) % n, True)
+        ring_all(half)
+
+        def evens(i, carry):
+            compute(0, (y + n + (i + 3) // 2 * (1 - 2 * ((i + 1) % 2))) % n, True)
             return carry
 
-        lax.fori_loop(0, n, odd, 0)
-        reduce([nothing] * half)
+        lax.fori_loop(0, n - 2, evens, 0)
+
+        def odds(first, last):
+            def body(i, carry):
+                compute(1, i, True)
+                return carry
+
+            lax.fori_loop(first, last, body, 0)
+
+        def index(k, p):
+            return p % (SUBS // 2) if k == 1 else SUBS // 2 + (k - 2) * SUBS + p
+
+        def sibling_states(par):
+            for i in range(n):
+                part = RB.at[par, i]
+                rcopy(
+                    part, part, p_send.at[par * n + i], p_recv.at[par * n + i], sib
+                ).wait_recv()
+
+        def ring_send(par, d, k, p, states):
+            i = index(k, p)
+            MS[par, d, i] = packed(merge(states)).reshape(per, heads, -1)
+            ss, rs = r_send.at[par, d, i], r_recv.at[par, d, i]
+            put(MS.at[par, d, i], RR.at[par, d, i], ss, rs, neighbour[par][d])
+
+        def ring_recv(par, d, k, p):
+            i = index(k, p)
+            part = RR.at[par, d, i]
+            rcopy(part, part, r_send.at[par, d, i], r_recv.at[par, d, i], sib).wait_recv()
+            return [opened(RR[par, d, i].reshape(rows, -1))]
+
+        def open_ring(par):
+            for p in range(SUBS // 2):
+                for d in range(2):
+                    q = halves(d)[1][p]
+                    ring_send(par, d, 1, q, both(par, goal(par, d, half), q))
+            for p in range(SUBS // 2):
+                for d in range(2):
+                    q = halves(d)[0][p]
+                    ring_send(par, d, 2, q, both(par, goal(par, d, half - 1), q))
+
+        def ring_step(pars, ks, js):
+            for j in js:
+                for par, k in zip(pars, ks):
+                    for d in range(2):
+                        p = (halves(d)[0] + halves(d)[1])[j]
+                        own = both(par, goal(par, d, half + 1 - k), p)
+                        ring_send(par, d, k, p, own + ring_recv(par, d, k - 1, p))
+
+        def close_ring(par):
+            for p in range(SUBS):
+                own = both(par, mid[par], p)
+                state = own + ring_recv(par, 0, half, p) + ring_recv(par, 1, half, p)
+                M2[par, ps(p)] = packed(merge(state)).reshape(per, heads, -1)
+            for k in far:
+                if par == 0:
+                    o, dev = (x + k) % n, at((x + k) % n, y, 0)
+                else:
+                    o, dev = (y + k) % n, at(x, (y + k) % n, 1)
+                put(M2.at[par, o], FB.at[k], f_send.at[par, k], f_recv.at[k], dev)
+            if par == 0:
+                put(M2.at[0, x], FB.at[0], f_send.at[0, 0], f_recv.at[0], sib)
+
+        late = range(SUBS // 2, SUBS)
+        every = range(SUBS)
+        sibling_states(0)
+        open_ring(0)
+        odds(0, 5)
+        ring_step((0,), (2,), late)
+        odds(5, n)
+        sibling_states(1)
+        open_ring(1)
+        ring_step((0,), (3,), every)
+        ring_step((1,), (2,), late)
+        ring_step((0, 1), (4, 3), every)
+        close_ring(0)
+        ring_step((1,), (4,), every)
+        close_ring(1)
+        states = [opened(M2[1, y])]
+        for k in far:
+            rcopy(FB.at[k], FB.at[k], f_send.at[1, k], f_recv.at[k], sib).wait_recv()
+            states.append(opened(FB[k]))
+        owned(states)
         for cp in out:
             cp.wait_send()
 
@@ -392,27 +403,33 @@
                     rcopy(part, part, d_send.at[par, d, i], d_recv.at[par, d, i], sib).wait_recv()
 
         rcopy(TB, TB, o_send.at[2], o_recv.at[2], sib).wait_recv()
-        build_table()
+        built = build_table()
         cl.wait()
         cr.wait()
         arrived(0, 0)
-        compute(0, y, True)
+        built.wait()
+        compute(0, y, False)
         for k in range(1, half + 1):
             arrived(0, k)
-            compute(0, (y + n - k) % n, True)
+            compute(0, (y + n - k) % n, False)
             if k < half:
-                compute(0, (y + k) % n, True)
+                compute(0, (y + k) % n, False)
         for k in range(half + 1):
             arrived(1, k)
 
-        def odds(first, last):
-            def body(i, carry):
-                compute(1, i, False)
-                return carry
-
-            return lambda: lax.fori_loop(first, last, body, 0) and None
-
-        reduce([odds(0, 3 * n // 4), odds(3 * n // 4, n)] + [nothing] * (half - 2))
+        def body(i, carry):
+            compute(1, i, False)
+            return carry
+
+        lax.fori_loop(0, n, body, 0)
+        states = []
+        for k in far + [0]:
+            rcopy(FB.at[k], FB.at[k], f_send.at[0, k], f_recv.at[k], sib).wait_recv()
+            states.append(opened(FB[k]))
+        owned(states)
+        for i in range(2 * n):
+            part = SB.at[i // n, i % n]
+            rcopy(part, part, p_send.at[i], p_recv.at[i], sib).wait_send()
         put_a.wait_send()
         put_t.wait_send()
 
@@ -425,7 +442,8 @@
     rope_w = q_rope.shape[2]
     slots, page, _ = cache_latent.shape
     width = lat_w + STAT
-    half = n // 2
+    half, per = n // 2, n // SUBS
+    messages = (half - 1) * SUBS + SUBS // 2
     any_spec = pl.BlockSpec(memory_space=pl.ANY)
     dma = pltpu.SemaphoreType.DMA
     out = pl.pallas_call(
@@ -438,14 +456,14 @@
             pltpu.VMEM(cache_rope.shape, bf16),
             pltpu.VMEM((2, n, n, heads, width), bf16),
             pltpu.VMEM((2, n, 8, 128), jnp.int32),
-            pltpu.VMEM((n, n, heads, width), bf16),
-            pltpu.VMEM((n, n, heads, width), bf16),
-            pltpu.VMEM((n, n, heads, lat_w), f32),
-            pltpu.VMEM((n, n, heads, STAT), f32),
-            pltpu.VMEM((n, n, heads, STAT), f32),
-            pltpu.VMEM((2, n - 1, half, heads, width), bf16),
-            pltpu.VMEM((2, n - 1, half, heads, width), bf16),
-            pltpu.VMEM((n, heads, width), bf16),
+            pltpu.VMEM((2, n, n, heads, width), bf16),
+            pltpu.VMEM((2, n, n, heads, width), bf16),
+            pltpu.VMEM((2, n, n, heads, lat_w), f32),
+            pltpu.VMEM((2, n, n, heads, STAT), f32),
+            pltpu.VMEM((2, n, n, heads, STAT), f32),
+            pltpu.VMEM((2, 2, messages, per, heads, width), bf16),
+            pltpu.VMEM((2, 2, messages, per, heads, width), bf16),
+            pltpu.VMEM((2, n, heads, width), bf16),
             pltpu.VMEM((n, heads, width), bf16),
             pltpu.VMEM((heads, width), bf16),
             pltpu.VMEM((8, 128), jnp.int32),
@@ -458,9 +476,9 @@
             dma((2, 2, half * SUBS)), dma((2, 2, half * SUBS)),
             dma((2, 2, half * SUBS)), dma((2, 2, half * SUBS)),
             dma((3,)), dma((3,)),
-            dma((n,)), dma((n,)),
-            dma((2, n - 1)), dma((2, n - 1)),
-            dma((n,)), dma((n,)),
+            dma((2 * n,)), dma((2 * n,)),
+            dma((2, 2, messages)), dma((2, 2, messages)),
+            dma((2, n)), dma((n,)),
         ],
         compiler_params=pltpu.CompilerParams(
             collective_id=0, has_side_effects=True, vmem_limit_bytes=57 * 1024 * 1024
@@ -471,7 +489,7 @@
 
 def solution(mesh):
     n = mesh.shape["head"]
-    assert mesh.shape["seq"] == 2 * n and n % 2 == 0
+    assert n == 8 and mesh.shape["seq"] == 2 * n
     placed = (
         P(("grp", "seq"), "head", None),
         P(("grp", "seq"), "head", None),

time: 75.9 us -> 80.2 us (1.057)
  Pallas kernels: 73.7 us -> 78 us
    pallas_call x1, Pallas kernels: 73.7 us -> 78 us  [on_device(): pl.pallas_call(functools.partial(kernel, n, heads, lat_w, rope_w, page, s...]
where the time goes in v4:
time: 80.2 us; the launch traced here: 79.9 us
  Pallas kernels  78 us (97%)
  local copies, waits for them, and re-layouts  1.32 us (2%)
    pallas_call x1, Pallas kernels, on_device(): pl.pallas_call(functools.partial(kernel, n, heads, lat_w, rope_w, page, s...  78 us

profile of v4, /device:TPU:513, one launch (start us, length us, event | category | flops | bytes accessed | tf_op | source)
XLA Modules:
  0.0 79.9 jit_solution(17225065514759254605)
XLA Ops:
  0.7 78.0 %shard_map.64 = bf16[16,512]{1,0:T(8,128)(2,1)} custom-call(bf16[1,16,512]{2,1,0:T(8,128)(2,1)} %ql_hbm.1, bf16[1,16,64]{2,1,0:T(8,128)(2,1)} %qr_hbm.1, bf16[36,128,512]{2,1,0:T(8,128)(2,1)} %lat_hbm.1, bf16[36,64,128]{2,1,0:T(8,128)(2,1)} %rope_hbm.1, s32[1,512]{1,0:T(1,128)} %pt_hbm.1, s32[1]{0:T(128)S(6)} %copy.8.len_ref), custom_call_target="tpu_custom_call" | custom-call | tf_op jit(solution)/shard_map/pallas_call | solution.py:449
  78.6 1.3 %copy.9 = bf16[1,16,512]{2,1,0:T(8,128)(2,1)} copy(bf16[1,16,512]{2,1,0:T(8,128)(2,1)} %bitcast.1) | data formatting | bytes 32768

commit v5 on v3

--- a/solution.py
+++ b/solution.py
@@ -121,28 +121,24 @@
         codes = TB[...].reshape(n * 16, 128)
         ok = (codes >= first) & (codes < first + slots * 256)
         key = jnp.where(ok, codes - first, -1).T
+        keys = [key] + [pltpu.roll(key, 128 - r, 1) for r in range(1, entries)]
         row = lax.broadcasted_iota(jnp.int32, (8, 128), 0)
-        lane = lax.broadcasted_iota(jnp.int32, (8, 128), 1)
         res = jnp.full((8, 128), -1, jnp.int32)
         for j in range(MOST):
-            m = key
-            size = key.shape[0]
+            m = functools.reduce(jnp.maximum, keys)
+            size = m.shape[0]
             while size > 8:
                 size //= 2
                 m = jnp.maximum(m[:size], m[size:])
             for r in (4, 2, 1):
                 m = jnp.maximum(m, pltpu.roll(m, r, 0))
-            for bit in (1, 2, 4):
-                other = jnp.where(
-                    (lane & bit) > 0, pltpu.roll(m, bit, 1), pltpu.roll(m, 128 - bit, 1)
-                )
-                m = jnp.maximum(m, other)
             res = jnp.where(row == j, m, res)
-            key = jnp.where(key == jnp.concatenate([m] * (n * 2), axis=0), -1, key)
+            full = jnp.concatenate([m] * (n * 2), axis=0)
+            keys = [jnp.where(v == full, -1, v) for v in keys]
         tvm[...] = res
         cp = pltpu.make_async_copy(tvm, tsm, loc.at[5])
         cp.start()
-        cp.wait()
+        return cp
 
     def stats(top, total):
         hi = total.astype(bf16)
@@ -194,7 +190,7 @@
             dst = RB.at[yy] if par == 0 else RB.at[:, yy]
             rcopy(SB.at[yy], dst, p_send.at[yy], p_recv.at[yy], sib).start()
 
-    rows = half * heads
+    rows = per * heads
     er = lax.broadcasted_iota(jnp.int32, (STAT, 2 * STAT), 0)
     ec = lax.broadcasted_iota(jnp.int32, (STAT, 2 * STAT), 1)
     spread = jnp.where(
@@ -217,29 +213,26 @@
         tiles, top, total = state
         return jnp.concatenate([t.astype(bf16) for t in tiles] + [stats(top, total)], axis=1)
 
-    def hs(h):
-        return pl.ds(h * half, half)
-
-    def local(idx, h):
-        v = LM[idx, hs(h)].reshape(rows, lat_w)
+    def ps(p):
+        return pl.ds(p * per, per)
+
+    def both(idx, p):
+        v = LM[idx, ps(p)].reshape(rows, lat_w)
         tiles = [v[:, j * 128 : (j + 1) * 128] for j in range(lanes)]
-        return tiles, LT[idx, hs(h)].reshape(rows, STAT), LS[idx, hs(h)].reshape(rows, STAT)
-
-    def both(idx, h):
-        return merge([local(idx, h), opened(RB[idx, hs(h)].reshape(rows, -1))])
-
-    def premerge(idx, h):
-        tiles, top, total = both(idx, h)
-        LM[idx, hs(h)] = jnp.concatenate(tiles, axis=1).reshape(half, heads, lat_w)
-        LT[idx, hs(h)] = top.reshape(half, heads, STAT)
-        LS[idx, hs(h)] = total.reshape(half, heads, STAT)
+        top = LT[idx, ps(p)].reshape(rows, STAT)
+        total = LS[idx, ps(p)].reshape(rows, STAT)
+        return [(tiles, top, total), opened(RB[idx, ps(p)].reshape(rows, -1))]
 
     def goal(d, k):
         return (b + k) % n if d == 0 else (b + n - k) % n
 
     nxt = (dev_b((b + 1) % n), dev_b((b + n - 1) % n))
-
-    def reduce(gaps):
+    halves = (
+        (tuple(range(SUBS // 2, SUBS)), tuple(range(SUBS // 2))),
+        (tuple(range(SUBS // 2)), tuple(range(SUBS // 2, SUBS))),
+    )
+
+    def reduce():
         out = []
 
         def put(src, dst, ss, rs, dev):
@@ -247,60 +240,64 @@
             cp.start()
             out.append(cp)
 
-        def ring_send(d, i, state):
-            MS[d, i] = packed(state).reshape(half, heads, -1)
-            put(MS.at[d, i], RR.at[d, i], r_send.at[d, i], r_recv.at[d, i], nxt[d])
-
-        def ring_recv(d, i):
-            rcopy(RR.at[d, i], RR.at[d, i], r_send.at[d, i], r_recv.at[d, i], sib).wait_recv()
-            return opened(RR[d, i].reshape(rows, -1))
-
-        def pre(k):
-            for d in range(2 if k else 1):
-                for h in range(2):
-                    premerge(goal(d, k), h)
+        def index(k, p):
+            return p % (SUBS // 2) if k == 1 else SUBS // 2 + (k - 2) * SUBS + p
+
+        def wait(d, k, p):
+            i = index(k, p)
+            part = RR.at[d, i]
+            rcopy(part, part, r_send.at[d, i], r_recv.at[d, i], sib).wait_recv()
+
+        def got(d, k, p):
+            return [opened(RR[d, index(k, p)].reshape(rows, -1))]
+
+        def step(k, subs, arrives):
+            states = [both(goal(d, half + 1 - k), subs[d]) for d in range(2)]
+            if arrives:
+                for d in range(2):
+                    wait(d, k - 1, subs[d])
+                states = [states[d] + got(d, k - 1, subs[d]) for d in range(2)]
+            full = [packed(merge(v)) for v in states]
+            for d in range(2):
+                MS[d, index(k, subs[d])] = full[d].reshape(per, heads, -1)
+            for d in range(2):
+                i = index(k, subs[d])
+                put(MS.at[d, i], RR.at[d, i], r_send.at[d, i], r_recv.at[d, i], nxt[d])
 
         for i in range(n):
             rcopy(RB.at[i], RB.at[i], p_send.at[i], p_recv.at[i], sib).wait_recv()
-        for d in range(2):
-            ring_send(d, 0, both(goal(d, half), d))
-        for d in range(2):
-            ring_send(d, 2 - d, both(goal(d, half - 1), 1 - d))
-        for d in range(2):
-            premerge(goal(d, half - 1), d)
-        gaps[0]()
-        for d in range(2):
-            ring_send(d, 1 + d, merge([local(goal(d, half - 1), d), ring_recv(d, 0)]))
+        first, late = [tuple(zip(halves[0][h], halves[1][h])) for h in range(2)]
+        for subs in late:
+            step(1, subs, False)
+        for subs in first:
+            step(2, subs, False)
+        for subs in late:
+            step(2, subs, True)
         for k in range(3, half + 1):
-            pre(half + 1 - k)
-            gaps[k - 2]()
-            for j in range(2):
+            for subs in first + late:
+                step(k, subs, True)
+        for j in range(0, SUBS, 2):
+            states = [both(b, p) for p in (j, j + 1)]
+            for p in (j, j + 1):
                 for d in range(2):
-                    h = 1 - d if j == 0 else d
-                    i = 1 + 2 * (k - 2) + h
-                    ring_send(d, i, merge([local(goal(d, half + 1 - k), h), ring_recv(d, i - 2)]))
-        pre(0)
-        gaps[half - 1]()
-        for h in range(2):
-            i = 1 + 2 * (half - 2) + h
-            state = merge([local(b, h), ring_recv(0, i), ring_recv(1, i)])
-            M2[hs(h)] = packed(state).reshape(half, heads, -1)
+                    wait(d, half, p)
+            full = [
+                packed(merge(v + got(0, half, p) + got(1, half, p)))
+                for v, p in zip(states, (j, j + 1))
+            ]
+            for v, p in zip(full, (j, j + 1)):
+                M2[ps(p)] = v.reshape(per, heads, -1)
         for k in far:
             o = (a + k) % n
             put(M2.at[o], FB.at[k], f_send.at[k], f_recv.at[k], dev_a(o))
-        states = [opened(M2[a])]
         for k in far:
             rcopy(FB.at[k], FB.at[k], f_send.at[k], f_recv.at[k], sib).wait_recv()
-            states.append(opened(FB[k]))
-        tiles, top, total = merge(states)
+        tiles, top, total = merge([opened(M2[a])] + [opened(FB[k]) for k in far])
         out_ref[...] = jnp.concatenate([(t / total).astype(bf16) for t in tiles], axis=1)
         for i in range(n):
             rcopy(SB.at[i], SB.at[i], p_send.at[i], p_recv.at[i], sib).wait_send()
         for cp in out:
             cp.wait_send()
-
-    def nothing():
-        return
 
     @pl.when(c == 1)
     def _():
@@ -329,15 +326,6 @@
                     put(part, part, g_send.at[par, d, p], g_recv.at[par, d, p], neighbour[par][d])
             part = QB.at[par, mid[par]]
             put(part, part, o_send.at[par], o_recv.at[par], sib)
-        for par in (1, 0):
-            for k in far + ([0] if par == 0 else []):
-                part = TB.at[par, (y + n - k) % n]
-                rcopy(part, part, t_send.at[k], t_recv.at[par, k], sib).wait_recv()
-        put(TB, TB, o_send.at[2], o_recv.at[2], sib)
-        build_table()
-        cl.wait()
-        cr.wait()
-
         def ring_sub(k, j):
             for par in (1, 0):
                 for d in range(2):
@@ -351,24 +339,38 @@
                         put(part, part, ss, rs, neighbour[par][d])
                     put(part, part, d_send.at[par, d, i], d_recv.at[par, d, i], sib)
 
-        compute(0, y, False)
-        rest = [(y + half) % n]
-        for k in range(half - 1, 0, -1):
-            rest += [(y + n - k) % n, (y + k) % n]
-        for k in range(1, half + 1):
+        def ring_all(k):
             for j in range(subs_at(k)):
                 ring_sub(k, j)
-            if k < half:
-                compute(0, rest.pop(), False)
-        while rest:
-            compute(0, rest.pop(), False)
+
+        ring_all(1)
+        for par in (1, 0):
+            for k in far + ([0] if par == 0 else []):
+                part = TB.at[par, (y + n - k) % n]
+                rcopy(part, part, t_send.at[k], t_recv.at[par, k], sib).wait_recv()
+        put(TB, TB, o_send.at[2], o_recv.at[2], sib)
+        built = build_table()
+        cl.wait()
+        cr.wait()
+        ring_all(2)
+        built.wait()
+        compute(0, y, False)
+        ring_all(3)
+        compute(0, (y + 1) % n, False)
+        ring_all(half)
+
+        def evens(i, carry):
+            compute(0, (y + n + (i + 3) // 2 * (1 - 2 * ((i + 1) % 2))) % n, False)
+            return carry
+
+        lax.fori_loop(0, n - 2, evens, 0)
 
         def odd(i, carry):
             compute(1, i, True)
             return carry
 
         lax.fori_loop(0, n, odd, 0)
-        reduce([nothing] * half)
+        reduce()
         for cp in out:
             cp.wait_send()
 
@@ -392,10 +394,11 @@
                     rcopy(part, part, d_send.at[par, d, i], d_recv.at[par, d, i], sib).wait_recv()
 
         rcopy(TB, TB, o_send.at[2], o_recv.at[2], sib).wait_recv()
-        build_table()
+        built = build_table()
         cl.wait()
         cr.wait()
         arrived(0, 0)
+        built.wait()
         compute(0, y, True)
         for k in range(1, half + 1):
             arrived(0, k)
@@ -405,14 +408,12 @@
         for k in range(half + 1):
             arrived(1, k)
 
-        def odds(first, last):
-            def body(i, carry):
-                compute(1, i, False)
-                return carry
-
-            return lambda: lax.fori_loop(first, last, body, 0) and None
-
-        reduce([odds(0, 3 * n // 4), odds(3 * n // 4, n)] + [nothing] * (half - 2))
+        def odd(i, carry):
+            compute(1, i, False)
+            return carry
+
+        lax.fori_loop(0, n, odd, 0)
+        reduce()
         put_a.wait_send()
         put_t.wait_send()
 
@@ -425,7 +426,8 @@
     rope_w = q_rope.shape[2]
     slots, page, _ = cache_latent.shape
     width = lat_w + STAT
-    half = n // 2
+    half, per = n // 2, n // SUBS
+    messages = (half - 1) * SUBS + SUBS // 2
     any_spec = pl.BlockSpec(memory_space=pl.ANY)
     dma = pltpu.SemaphoreType.DMA
     out = pl.pallas_call(
@@ -443,8 +445,8 @@
             pltpu.VMEM((n, n, heads, lat_w), f32),
             pltpu.VMEM((n, n, heads, STAT), f32),
             pltpu.VMEM((n, n, heads, STAT), f32),
-            pltpu.VMEM((2, n - 1, half, heads, width), bf16),
-            pltpu.VMEM((2, n - 1, half, heads, width), bf16),
+            pltpu.VMEM((2, messages, per, heads, width), bf16),
+            pltpu.VMEM((2, messages, per, heads, width), bf16),
             pltpu.VMEM((n, heads, width), bf16),
             pltpu.VMEM((n, heads, width), bf16),
             pltpu.VMEM((heads, width), bf16),
@@ -459,7 +461,7 @@
             dma((2, 2, half * SUBS)), dma((2, 2, half * SUBS)),
             dma((3,)), dma((3,)),
             dma((n,)), dma((n,)),
-            dma((2, n - 1)), dma((2, n - 1)),
+            dma((2, messages)), dma((2, messages)),
             dma((n,)), dma((n,)),
         ],
         compiler_params=pltpu.CompilerParams(
@@ -471,7 +473,7 @@
 
 def solution(mesh):
     n = mesh.shape["head"]
-    assert mesh.shape["seq"] == 2 * n and n % 2 == 0
+    assert n == 8 and mesh.shape["seq"] == 2 * n
     placed = (
         P(("grp", "seq"), "head", None),
         P(("grp", "seq"), "head", None),

time: 75.9 us -> 71.9 us (0.947)
  Pallas kernels: 73.7 us -> 69.3 us
    pallas_call x1, Pallas kernels: 73.7 us -> 69.3 us  [on_device(): pl.pallas_call(functools.partial(kernel, n, heads, lat_w, rope_w, page, s...]
where the time goes in v5:
time: 71.9 us; the launch traced here: 71.3 us
  Pallas kernels  69.3 us (96%)
  local copies, waits for them, and re-layouts  1.32 us (2%)
    pallas_call x1, Pallas kernels, on_device(): pl.pallas_call(functools.partial(kernel, n, heads, lat_w, rope_w, page, s...  69.3 us

profile of v5, /device:TPU:513, one launch (start us, length us, event | category | flops | bytes accessed | tf_op | source)
XLA Modules:
  0.0 71.3 jit_solution(4449630523621411377)
XLA Ops:
  0.7 69.3 %shard_map.64 = bf16[16,512]{1,0:T(8,128)(2,1)} custom-call(bf16[1,16,512]{2,1,0:T(8,128)(2,1)} %ql_hbm.1, bf16[1,16,64]{2,1,0:T(8,128)(2,1)} %qr_hbm.1, bf16[36,128,512]{2,1,0:T(8,128)(2,1)} %lat_hbm.1, bf16[36,64,128]{2,1,0:T(8,128)(2,1)} %rope_hbm.1, s32[1,512]{1,0:T(1,128)} %pt_hbm.1, s32[1]{0:T(128)S(6)} %copy.8.len_ref), custom_call_target="tpu_custom_call" | custom-call | tf_op jit(solution)/shard_map/pallas_call | solution.py:433
  70.0 1.3 %copy.9 = bf16[1,16,512]{2,1,0:T(8,128)(2,1)} copy(bf16[1,16,512]{2,1,0:T(8,128)(2,1)} %bitcast.1) | data formatting | bytes 32768

commit v6 on v5

--- a/solution.py
+++ b/solution.py
@@ -147,7 +147,7 @@
         st = jnp.where(lane == 0, top, jnp.where(lane == 1, hi.astype(f32), lo.astype(f32)))
         return st.astype(bf16)
 
-    def compute(par, yy, own):
+    def attend(par, yy):
         q = (QB[0, yy] if par == 0 else QB[1, :, yy]).reshape(n * heads, -1)
         ql, qr = q[:, :lat_w], q[:, lat_w : lat_w + rope_w]
         pages, ropes, counts = [], [], []
@@ -174,6 +174,10 @@
         mixed = jnp.dot(w, keys, preferred_element_type=f32)
         top = jnp.broadcast_to(top, (n * heads, STAT))
         total = jnp.broadcast_to(total, (n * heads, STAT))
+        return mixed, top, total
+
+    def keep(par, yy, own, state):
+        mixed, top, total = state
         shape = (n, heads, -1)
 
         if own and par == 0:
@@ -187,8 +191,18 @@
         else:
             full = jnp.concatenate([mixed.astype(bf16), stats(top, total)], axis=1)
             SB[yy] = full.reshape(shape)
-            dst = RB.at[yy] if par == 0 else RB.at[:, yy]
-            rcopy(SB.at[yy], dst, p_send.at[yy], p_recv.at[yy], sib).start()
+
+    def push(par, yy):
+        dst = RB.at[yy] if par == 0 else RB.at[:, yy]
+        rcopy(SB.at[yy], dst, p_send.at[yy], p_recv.at[yy], sib).start()
+
+    def compute(par, own, *seqs):
+        states = [attend(par, yy) for yy in seqs]
+        for yy, state in zip(seqs, states):
+            keep(par, yy, own, state)
+        if not own:
+            for yy in seqs:
+                push(par, yy)
 
     rows = per * heads
     er = lax.broadcasted_iota(jnp.int32, (STAT, 2 * STAT), 0)
@@ -343,7 +357,6 @@
             for j in range(subs_at(k)):
                 ring_sub(k, j)
 
-        ring_all(1)
         for par in (1, 0):
             for k in far + ([0] if par == 0 else []):
                 part = TB.at[par, (y + n - k) % n]
@@ -352,24 +365,23 @@
         built = build_table()
         cl.wait()
         cr.wait()
+        built.wait()
+        compute(0, False, y)
+        ring_all(1)
+        compute(0, False, (y + 1) % n)
         ring_all(2)
-        built.wait()
-        compute(0, y, False)
+        compute(0, False, (y + n - 1) % n)
         ring_all(3)
-        compute(0, (y + 1) % n, False)
+        compute(0, False, (y + 2) % n)
         ring_all(half)
-
-        def evens(i, carry):
-            compute(0, (y + n + (i + 3) // 2 * (1 - 2 * ((i + 1) % 2))) % n, False)
+        compute(0, False, (y + n - 2) % n, (y + half) % n)
+        compute(0, False, (y + n - 3) % n, (y + 3) % n)
+
+        def odd(i, carry):
+            compute(1, True, 2 * i, 2 * i + 1)
             return carry
 
-        lax.fori_loop(0, n - 2, evens, 0)
-
-        def odd(i, carry):
-            compute(1, i, True)
-            return carry
-
-        lax.fori_loop(0, n, odd, 0)
+        lax.fori_loop(0, n // 2, odd, 0)
         reduce()
         for cp in out:
             cp.wait_send()
@@ -399,20 +411,21 @@
         cr.wait()
         arrived(0, 0)
         built.wait()
-        compute(0, y, True)
+        compute(0, True, y)
         for k in range(1, half + 1):
             arrived(0, k)
-            compute(0, (y + n - k) % n, True)
             if k < half:
-                compute(0, (y + k) % n, True)
+                compute(0, True, (y + n - k) % n, (y + k) % n)
+            else:
+                compute(0, True, (y + half) % n)
         for k in range(half + 1):
             arrived(1, k)
 
         def odd(i, carry):
-            compute(1, i, False)
+            compute(1, False, 2 * i, 2 * i + 1)
             return carry
 
-        lax.fori_loop(0, n, odd, 0)
+        lax.fori_loop(0, n // 2, odd, 0)
         reduce()
         put_a.wait_send()
         put_t.wait_send()

time: 71.9 us -> 71.2 us (level)
  Pallas kernels: 69.3 us -> 68.4 us
    pallas_call x1, Pallas kernels: 69.3 us -> 68.4 us  [on_device(): pl.pallas_call(functools.partial(kernel, n, heads, lat_w, rope_w, page, s...]
where the time goes in v6:
time: 71.2 us; the launch traced here: 70.4 us
  Pallas kernels  68.4 us (96%)
  local copies, waits for them, and re-layouts  1.32 us (2%)
    pallas_call x1, Pallas kernels, on_device(): pl.pallas_call(functools.partial(kernel, n, heads, lat_w, rope_w, page, s...  68.4 us

profile of v6, /device:TPU:513, one launch (start us, length us, event | category | flops | bytes accessed | tf_op | source)
XLA Modules:
  0.0 70.4 jit_solution(13364126849565824144)
XLA Ops:
  0.7 68.4 %shard_map.64 = bf16[16,512]{1,0:T(8,128)(2,1)} custom-call(bf16[1,16,512]{2,1,0:T(8,128)(2,1)} %ql_hbm.1, bf16[1,16,64]{2,1,0:T(8,128)(2,1)} %qr_hbm.1, bf16[36,128,512]{2,1,0:T(8,128)(2,1)} %lat_hbm.1, bf16[36,64,128]{2,1,0:T(8,128)(2,1)} %rope_hbm.1, s32[1,512]{1,0:T(1,128)} %pt_hbm.1, s32[1]{0:T(128)S(6)} %copy.8.len_ref), custom_call_target="tpu_custom_call" | custom-call | tf_op jit(solution)/shard_map/pallas_call | solution.py:446
  69.1 1.3 %copy.9 = bf16[1,16,512]{2,1,0:T(8,128)(2,1)} copy(bf16[1,16,512]{2,1,0:T(8,128)(2,1)} %bitcast.1) | data formatting | bytes 32768

commit v7 on v6

--- a/solution.py
+++ b/solution.py
@@ -62,7 +62,7 @@
     partners = [at((x + k) % n, y, 1 - c) for k in far]
     partners += [at(x, (y + k) % n, 1 - c) for k in far]
     partners += [dev_a((a + k) % n) for k in far]
-    partners += [dev_b((b + 1) % n), dev_b((b + n - 1) % n), sib]
+    partners += [dev_b((b + k) % n) for k in (1, 2, n - 2, n - 1)] + [sib]
     for dev in partners:
         pl.semaphore_signal(bar, inc=1, device_id=dev, device_id_type=MESH)
 
@@ -240,13 +240,12 @@
     def goal(d, k):
         return (b + k) % n if d == 0 else (b + n - k) % n
 
-    nxt = (dev_b((b + 1) % n), dev_b((b + n - 1) % n))
     halves = (
         (tuple(range(SUBS // 2, SUBS)), tuple(range(SUBS // 2))),
         (tuple(range(SUBS // 2)), tuple(range(SUBS // 2, SUBS))),
     )
 
-    def reduce():
+    def reduce(gap):
         out = []
 
         def put(src, dst, ss, rs, dev):
@@ -255,7 +254,9 @@
             out.append(cp)
 
         def index(k, p):
-            return p % (SUBS // 2) if k == 1 else SUBS // 2 + (k - 2) * SUBS + p
+            return {4: p % (SUBS // 2), 3: SUBS // 2, 2: SUBS // 2 + SUBS, 1: SUBS // 2 + 2 * SUBS}[
+                k
+            ] + (p if k < half else 0)
 
         def wait(d, k, p):
             i = index(k, p)
@@ -265,38 +266,43 @@
         def got(d, k, p):
             return [opened(RR[d, index(k, p)].reshape(rows, -1))]
 
-        def step(k, subs, arrives):
-            states = [both(goal(d, half + 1 - k), subs[d]) for d in range(2)]
-            if arrives:
-                for d in range(2):
-                    wait(d, k - 1, subs[d])
-                states = [states[d] + got(d, k - 1, subs[d]) for d in range(2)]
+        def step(k, subs, comes=()):
+            states = [both(goal(d, k), subs[d]) for d in range(2)]
+            for d in range(2):
+                for g in comes:
+                    wait(d, g, subs[d])
+            for g in comes:
+                states = [states[d] + got(d, g, subs[d]) for d in range(2)]
             full = [packed(merge(v)) for v in states]
             for d in range(2):
                 MS[d, index(k, subs[d])] = full[d].reshape(per, heads, -1)
             for d in range(2):
-                i = index(k, subs[d])
-                put(MS.at[d, i], RR.at[d, i], r_send.at[d, i], r_recv.at[d, i], nxt[d])
+                i, hops = index(k, subs[d]), 2 - k % 2
+                dev = dev_b((b + (hops if d == 0 else n - hops)) % n)
+                put(MS.at[d, i], RR.at[d, i], r_send.at[d, i], r_recv.at[d, i], dev)
 
         for i in range(n):
             rcopy(RB.at[i], RB.at[i], p_send.at[i], p_recv.at[i], sib).wait_recv()
         first, late = [tuple(zip(halves[0][h], halves[1][h])) for h in range(2)]
         for subs in late:
-            step(1, subs, False)
+            step(4, subs)
+        for subs in first + late:
+            step(3, subs)
+        for subs in first + late:
+            step(1, subs)
+        gap()
         for subs in first:
-            step(2, subs, False)
+            step(2, subs, (3,))
         for subs in late:
-            step(2, subs, True)
-        for k in range(3, half + 1):
-            for subs in first + late:
-                step(k, subs, True)
+            step(2, subs, (3, 4))
         for j in range(0, SUBS, 2):
             states = [both(b, p) for p in (j, j + 1)]
-            for p in (j, j + 1):
-                for d in range(2):
-                    wait(d, half, p)
+            for k in (1, 2):
+                for p in (j, j + 1):
+                    for d in range(2):
+                        wait(d, k, p)
             full = [
-                packed(merge(v + got(0, half, p) + got(1, half, p)))
+                packed(merge(v + [g for k in (1, 2) for d in range(2) for g in got(d, k, p)]))
                 for v, p in zip(states, (j, j + 1))
             ]
             for v, p in zip(full, (j, j + 1)):
@@ -382,7 +388,7 @@
             return carry
 
         lax.fori_loop(0, n // 2, odd, 0)
-        reduce()
+        reduce(lambda: None)
         for cp in out:
             cp.wait_send()
 
@@ -426,7 +432,7 @@
             return carry
 
         lax.fori_loop(0, n // 2, odd, 0)
-        reduce()
+        reduce(lambda: None)
         put_a.wait_send()
         put_t.wait_send()
 
@@ -445,7 +451,7 @@
     dma = pltpu.SemaphoreType.DMA
     out = pl.pallas_call(
         functools.partial(kernel, n, heads, lat_w, rope_w, page, slots),
-        out_shape=jax.ShapeDtypeStruct((heads, lat_w), bf16),
+        out_shape=pltpu.VMEM((heads, lat_w), bf16),
         in_specs=[any_spec] * 5 + [pl.BlockSpec(memory_space=pltpu.SMEM)],
         out_specs=pl.BlockSpec(memory_space=pltpu.VMEM),
         scratch_shapes=[

time: 71.2 us -> 68.2 us (0.958)
  Pallas kernels: 68.4 us -> 66.8 us
    pallas_call x1, Pallas kernels: 68.4 us -> 66.8 us  [on_device(): pl.pallas_call(functools.partial(kernel, n, heads, lat_w, rope_w, page, s...]
    unnamed x1, local copies, waits for them, and re-layouts: 1.32 us -> 0.61 us
where the time goes in v7:
time: 68.2 us; the launch traced here: 68.1 us
  Pallas kernels  66.8 us (98%)
    pallas_call x1, Pallas kernels, on_device(): pl.pallas_call(functools.partial(kernel, n, heads, lat_w, rope_w, page, s...  66.8 us

profile of v7, /device:TPU:513, one launch (start us, length us, event | category | flops | bytes accessed | tf_op | source)
XLA Modules:
  0.0 68.1 jit_solution(10815288305461902600)
XLA Ops:
  0.7 66.8 %shard_map.64 = bf16[16,512]{1,0:T(8,128)(2,1)S(1)} custom-call(bf16[1,16,512]{2,1,0:T(8,128)(2,1)} %ql_hbm.1, bf16[1,16,64]{2,1,0:T(8,128)(2,1)} %qr_hbm.1, bf16[36,128,512]{2,1,0:T(8,128)(2,1)} %lat_hbm.1, bf16[36,64,128]{2,1,0:T(8,128)(2,1)} %rope_hbm.1, s32[1,512]{1,0:T(1,128)} %pt_hbm.1, s32[1]{0:T(128)S(6)} %copy.9.len_ref), custom_call_target="tpu_custom_call" | custom-call | tf_op jit(solution)/shard_map/pallas_call | solution.py:452
  67.5 0.6 copy.8

commit v8 on v7

--- a/solution.py
+++ b/solution.py
@@ -13,6 +13,7 @@
 MOST = 4
 STAT = 128
 SUBS = 4
+GSUBS = 2
 bf16, f32 = jnp.bfloat16, jnp.float32
 
 
@@ -102,11 +103,11 @@
         send(town, TB.at[c, y], t_send.at[k], t_recv.at[c, k], at(x, (y + k) % n, 1))
 
     def part_of(par, idx, p):
-        return QB.at[par, idx, pl.ds(p * per, per)]
+        return QB.at[par, idx, pl.ds(p * (n // GSUBS), n // GSUBS)]
 
     order = (
-        tuple(range(SUBS)),
-        tuple(range(SUBS // 2, SUBS)) + tuple(range(SUBS // 2)),
+        tuple(range(GSUBS)),
+        tuple(range(GSUBS // 2, GSUBS)) + tuple(range(GSUBS // 2)),
     )
     mid = (y, x)
 
@@ -114,7 +115,7 @@
         return (mid[par] + n - k) % n if d == 0 else (mid[par] + k) % n
 
     def subs_at(k):
-        return SUBS // 2 if k == half else SUBS
+        return GSUBS // 2 if k == half else GSUBS
 
     def build_table():
         first = (sq * n + x) * slots * 256
@@ -245,7 +246,7 @@
         (tuple(range(SUBS // 2)), tuple(range(SUBS // 2, SUBS))),
     )
 
-    def reduce(gap):
+    def reduce(need):
         out = []
 
         def put(src, dst, ss, rs, dev):
@@ -281,16 +282,15 @@
                 dev = dev_b((b + (hops if d == 0 else n - hops)) % n)
                 put(MS.at[d, i], RR.at[d, i], r_send.at[d, i], r_recv.at[d, i], dev)
 
-        for i in range(n):
-            rcopy(RB.at[i], RB.at[i], p_send.at[i], p_recv.at[i], sib).wait_recv()
         first, late = [tuple(zip(halves[0][h], halves[1][h])) for h in range(2)]
-        for subs in late:
-            step(4, subs)
-        for subs in first + late:
-            step(3, subs)
-        for subs in first + late:
-            step(1, subs)
-        gap()
+        for j in range(2):
+            for i in need[j]:
+                rcopy(RB.at[i], RB.at[i], p_send.at[i], p_recv.at[i], sib).wait_recv()
+            step(4, late[j])
+            step(3, first[j])
+            step(3, late[j])
+            step(1, first[j])
+            step(1, late[j])
         for subs in first:
             step(2, subs, (3,))
         for subs in late:
@@ -339,7 +339,7 @@
                 src = (x + n - k) % n if par == 0 else (y + n - k) % n
                 part = QB.at[par, mid[par], src]
                 rcopy(part, part, a_send.at[k], a_recv.at[par, k], sib).wait_recv()
-            for j in range(SUBS):
+            for j in range(GSUBS):
                 for d in range(2):
                     p = order[d][j]
                     part = part_of(par, mid[par], p)
@@ -350,11 +350,11 @@
             for par in (1, 0):
                 for d in range(2):
                     p = order[d][j]
-                    i = (k - 1) * SUBS + p
+                    i = (k - 1) * GSUBS + p
                     part = part_of(par, origin(par, d, k), p)
                     rcopy(part, part, g_send.at[par, d, i], g_recv.at[par, d, i], sib).wait_recv()
-                    if k < half - 1 or (k == half - 1 and j < SUBS // 2):
-                        i2 = i + SUBS
+                    if k < half - 1 or (k == half - 1 and j < GSUBS // 2):
+                        i2 = i + GSUBS
                         ss, rs = g_send.at[par, d, i2], g_recv.at[par, d, i2]
                         put(part, part, ss, rs, neighbour[par][d])
                     put(part, part, d_send.at[par, d, i], d_recv.at[par, d, i], sib)
@@ -384,11 +384,12 @@
         compute(0, False, (y + n - 3) % n, (y + 3) % n)
 
         def odd(i, carry):
-            compute(1, True, 2 * i, 2 * i + 1)
+            first = 4 * (i % 2) + 2 * (i // 2)
+            compute(1, True, first, first + 1)
             return carry
 
         lax.fori_loop(0, n // 2, odd, 0)
-        reduce(lambda: None)
+        reduce(((0, 1, 4, 5), (2, 3, 6, 7)))
         for cp in out:
             cp.wait_send()
 
@@ -407,7 +408,7 @@
             for j in range(subs_at(k)):
                 for d in range(2):
                     p = order[d][j]
-                    i = (k - 1) * SUBS + p
+                    i = (k - 1) * GSUBS + p
                     part = part_of(par, origin(par, d, k), p)
                     rcopy(part, part, d_send.at[par, d, i], d_recv.at[par, d, i], sib).wait_recv()
 
@@ -428,11 +429,12 @@
             arrived(1, k)
 
         def odd(i, carry):
-            compute(1, False, 2 * i, 2 * i + 1)
+            first = 4 * (i % 2) + 2 * (i // 2)
+            compute(1, False, first, first + 1)
             return carry
 
         lax.fori_loop(0, n // 2, odd, 0)
-        reduce(lambda: None)
+        reduce((tuple(range(n)), ()))
         put_a.wait_send()
         put_t.wait_send()
 
@@ -476,8 +478,8 @@
             pltpu.SMEM((8, 128), jnp.int32),
             dma((6,)),
             dma((n,)), dma((2, n)), dma((n,)), dma((2, n)),
-            dma((2, 2, half * SUBS)), dma((2, 2, half * SUBS)),
-            dma((2, 2, half * SUBS)), dma((2, 2, half * SUBS)),
+            dma((2, 2, half * GSUBS)), dma((2, 2, half * GSUBS)),
+            dma((2, 2, half * GSUBS)), dma((2, 2, half * GSUBS)),
             dma((3,)), dma((3,)),
             dma((n,)), dma((n,)),
             dma((2, messages)), dma((2, messages)),

time: 68.2 us -> 67.5 us (0.990)
  no operation moved by 1% of the time
where the time goes in v8:
time: 67.5 us; the launch traced here: 67.4 us
  Pallas kernels  66.2 us (98%)
    pallas_call x1, Pallas kernels, on_device(): pl.pallas_call(functools.partial(kernel, n, heads, lat_w, rope_w, page, s...  66.2 us

profile of v8, /device:TPU:513, one launch (start us, length us, event | category | flops | bytes accessed | tf_op | source)
XLA Modules:
  0.0 67.4 jit_solution(1926318589375176387)
XLA Ops:
  0.7 66.2 %shard_map.64 = bf16[16,512]{1,0:T(8,128)(2,1)S(1)} custom-call(bf16[1,16,512]{2,1,0:T(8,128)(2,1)} %ql_hbm.1, bf16[1,16,64]{2,1,0:T(8,128)(2,1)} %qr_hbm.1, bf16[36,128,512]{2,1,0:T(8,128)(2,1)} %lat_hbm.1, bf16[36,64,128]{2,1,0:T(8,128)(2,1)} %rope_hbm.1, s32[1,512]{1,0:T(1,128)} %pt_hbm.1, s32[1]{0:T(128)S(6)} %copy.9.len_ref), custom_call_target="tpu_custom_call" | custom-call | tf_op jit(solution)/shard_map/pallas_call | solution.py:454
  66.8 0.6 copy.8

commit v9 on v8

--- a/solution.py
+++ b/solution.py
@@ -307,15 +307,21 @@
             ]
             for v, p in zip(full, (j, j + 1)):
                 M2[ps(p)] = v.reshape(per, heads, -1)
-        for k in far:
-            o = (a + k) % n
-            put(M2.at[o], FB.at[k], f_send.at[k], f_recv.at[k], dev_a(o))
+            for o in range(j * per, (j + 2) * per):
+                k = (o + n - a) % n
+
+                @pl.when(o != a)
+                def _(o=o, k=k):
+                    rcopy(M2.at[o], FB.at[k], f_send.at[k], f_recv.at[k], dev_a(o)).start()
+
         for k in far:
             rcopy(FB.at[k], FB.at[k], f_send.at[k], f_recv.at[k], sib).wait_recv()
         tiles, top, total = merge([opened(M2[a])] + [opened(FB[k]) for k in far])
         out_ref[...] = jnp.concatenate([(t / total).astype(bf16) for t in tiles], axis=1)
         for i in range(n):
             rcopy(SB.at[i], SB.at[i], p_send.at[i], p_recv.at[i], sib).wait_send()
+        for k in far:
+            rcopy(FB.at[k], FB.at[k], f_send.at[k], f_recv.at[k], sib).wait_send()
         for cp in out:
             cp.wait_send()
 

time: 67.5 us -> 66.7 us (0.988)
  Pallas kernels: 66.2 us -> 65.3 us
    pallas_call x1, Pallas kernels: 66.2 us -> 65.3 us  [on_device(): pl.pallas_call(functools.partial(kernel, n, heads, lat_w, rope_w, page, s...]
where the time goes in v9:
time: 66.7 us; the launch traced here: 66.6 us
  Pallas kernels  65.3 us (98%)
    pallas_call x1, Pallas kernels, on_device(): pl.pallas_call(functools.partial(kernel, n, heads, lat_w, rope_w, page, s...  65.3 us

profile of v9, /device:TPU:513, one launch (start us, length us, event | category | flops | bytes accessed | tf_op | source)
XLA Modules:
  0.0 66.6 jit_solution(3608309938618397317)
XLA Ops:
  0.7 65.3 %shard_map.64 = bf16[16,512]{1,0:T(8,128)(2,1)S(1)} custom-call(bf16[1,16,512]{2,1,0:T(8,128)(2,1)} %ql_hbm.1, bf16[1,16,64]{2,1,0:T(8,128)(2,1)} %qr_hbm.1, bf16[36,128,512]{2,1,0:T(8,128)(2,1)} %lat_hbm.1, bf16[36,64,128]{2,1,0:T(8,128)(2,1)} %rope_hbm.1, s32[1,512]{1,0:T(1,128)} %pt_hbm.1, s32[1]{0:T(128)S(6)} %copy.9.len_ref), custom_call_target="tpu_custom_call" | custom-call | tf_op jit(solution)/shard_map/pallas_call | solution.py:460
  65.9 0.6 copy.8
